TPU v7x, 32 devices: a whole 2x2x4 slice. The times are simulated.
32 devices in a mesh: dp: 32 (over z, y, x, core).
Axes of the slice: x: 2, y: 2, z: 4, core: 2. Of those that a mesh axis runs over, the one named last changes fastest.
Arguments:
- captions: bfloat16 [1024, 77, 768], P('dp'), may hold values from -6 to 6
- caption_layout: int32 [2, 1024], replicated, may hold values from 0 to 77, as said below
- images: bfloat16 [1024, 768], P('dp'), may hold values from -0.24 to 0.24
- w_query: bfloat16 [768, 768], replicated, may hold values from -0.21875 to 0.21875
- w_keyval: bfloat16 [768, 1536], replicated, may hold values from -0.21875 to 0.21875
- w_out: bfloat16 [768, 768], replicated, may hold values from -0.21875 to 0.21875
- w_up: bfloat16 [768, 3072], replicated, may hold values from -0.21875 to 0.21875
- w_down: bfloat16 [3072, 768], replicated, may hold values from -0.109375 to 0.109375
- w_proj: bfloat16 [768, 768], replicated, may hold values from -0.009114583 to 0.009114583
Outputs:
- image_grad: float32 [1024, 768], P('dp')
- text_grad: float32 [1024, 768], P('dp')
Inputs may be any that keep to these rules, and one draw needn't show every extreme that they name: `caption_layout`: row 0 holds each caption's token count; row 1 is 1 where the caption is encoded by the next index of dp (index 0 after the last) and 0 where by its own. Exactly 8 of each device's captions carry 1. The captions one device encodes (its own that carry 0 and those carrying 1 of the index before it) hold at most 2048 tokens together, exactly that many on some device.
All inputs are finite; a program needn't handle non-finite values.
Results may differ from a plain program's by a relative error of at most 0.018.
Values may be sent and summed in bfloat16 or wider, within the bound.
No kernel may reach another device: no remote copies, remote signals or barrier semaphores. Data moves between devices by JAX's collectives and lax.ppermute only.
A program may use at most 128 MiB of HBM per device.

v0:
```python
import math

import jax
import jax.numpy as jnp
from jax import lax
from jax.sharding import PartitionSpec as P

HEADS = 12
HAND = 8
TOK_CAP = 2048


LOGIT_SCALE = 100.0
EPS_NORM = 1e-05
EPS_UNIT = 1e-06


def from_behind(value, axis, steps):
    count = lax.axis_size(axis)
    pairs = [(source, (source + steps) % count) for source in range(count)]
    return lax.ppermute(value, axis, pairs)


def layer_norm(values):
    values = values.astype(jnp.float32)
    center = values - jnp.mean(values, axis=-1, keepdims=True)
    spread = jnp.mean(center * center, axis=-1, keepdims=True)
    return center * lax.rsqrt(spread + EPS_NORM)


def unit_rows(values):
    values = values.astype(jnp.float32)
    return values * lax.rsqrt(jnp.sum(values * values, axis=-1, keepdims=True) + EPS_UNIT)


def contract_first(left, right):
    return lax.dot_general(
        left, right, (((0,), (0,)), ((), ())), preferred_element_type=jnp.float32
    )


def contract_last(left, right):
    return lax.dot_general(
        left, right, (((1,), (1,)), ((), ())), preferred_element_type=jnp.float32
    )


def encode(token_rows, slot_starts, slot_lengths, weight_set):
    w_query, w_keyval, w_out, w_up, w_down, w_proj = weight_set
    total_rows, model_width = token_rows.shape
    head_dim = model_width // HEADS
    normed = layer_norm(token_rows).astype(jnp.bfloat16)
    keyval = jnp.dot(normed, w_keyval, preferred_element_type=jnp.float32).astype(jnp.bfloat16)
    last_row = jnp.clip(slot_starts + slot_lengths - 1, 0, total_rows - 1)
    query = jnp.dot(normed[last_row], w_query, preferred_element_type=jnp.float32).astype(
        jnp.bfloat16
    )
    key_heads = keyval[:, :model_width].reshape(total_rows, HEADS, head_dim)
    value_heads = keyval[:, model_width:].reshape(total_rows, HEADS, head_dim)
    query_heads = query.reshape(-1, HEADS, head_dim)
    scores = jnp.einsum("shd,rhd->hsr", query_heads, key_heads, preferred_element_type=jnp.float32)
    scores = scores / math.sqrt(head_dim)
    position = jnp.arange(total_rows)[None, :]
    inside = (position >= slot_starts[:, None]) & (position < (slot_starts + slot_lengths)[:, None])
    inside = jnp.where(slot_lengths[:, None] > 0, inside, position == 0)
    masked = jnp.where(inside[None], scores, -jnp.inf)
    peak = jnp.max(masked, axis=-1, keepdims=True)
    exponent = jnp.exp(masked - peak)
    attention = (exponent / jnp.sum(exponent, axis=-1, keepdims=True)).astype(jnp.bfloat16)
    mixed_heads = jnp.einsum(
        "hsr,rhd->shd", attention, value_heads, preferred_element_type=jnp.float32
    )
    mixed_heads = mixed_heads.astype(jnp.bfloat16).reshape(-1, model_width)
    residual = token_rows[last_row].astype(jnp.float32) + jnp.dot(
        mixed_heads, w_out, preferred_element_type=jnp.float32
    )
    residual = residual.astype(jnp.bfloat16)
    inner_norm = layer_norm(residual).astype(jnp.bfloat16)
    hidden = jax.nn.gelu(
        jnp.dot(inner_norm, w_up, preferred_element_type=jnp.float32), approximate=False
    )
    hidden = hidden.astype(jnp.bfloat16)
    final_rows = residual.astype(jnp.float32) + jnp.dot(
        hidden, w_down, preferred_element_type=jnp.float32
    )
    pooled = layer_norm(final_rows).astype(jnp.bfloat16)
    return jnp.dot(pooled, w_proj, preferred_element_type=jnp.float32).astype(jnp.bfloat16)


def hand_slots(handed_flags, slot_total):
    before = jnp.cumsum(handed_flags) - handed_flags
    slot_index = jnp.arange(slot_total)[:, None]
    picked = (handed_flags[None, :] == 1) & (before[None, :] == slot_index)
    caption_index = jnp.arange(handed_flags.shape[0])[None, :]
    source = jnp.sum(jnp.where(picked, caption_index, 0), axis=1)
    return (before, source, jnp.any(picked, axis=1))


def body(captions, caption_layout, images, w_query, w_keyval, w_out, w_up, w_down, w_proj):
    caption_count, context, model_width = captions.shape
    device_count = lax.axis_size("dp")
    device_index = lax.axis_index("dp")
    weight_set = (w_query, w_keyval, w_out, w_up, w_down, w_proj)
    own_lengths = lax.dynamic_slice_in_dim(
        caption_layout[0], device_index * caption_count, caption_count
    )
    image_unit = unit_rows(images).astype(jnp.bfloat16)
    all_images = lax.all_gather(image_unit, "dp", axis=0, tiled=True)
    own_flags = lax.dynamic_slice_in_dim(
        caption_layout[1], device_index * caption_count, caption_count
    )
    previous = (device_index + device_count - 1) % device_count
    prev_lengths = lax.dynamic_slice_in_dim(
        caption_layout[0], previous * caption_count, caption_count
    )
    prev_flags = lax.dynamic_slice_in_dim(
        caption_layout[1], previous * caption_count, caption_count
    )
    before, source, slot_live = hand_slots(own_flags, HAND)
    outgoing = jnp.take(captions, source, axis=0)
    incoming = from_behind(outgoing, "dp", 1)
    prev_before, prev_source, prev_live = hand_slots(prev_flags, HAND)
    incoming_lengths = jnp.where(prev_live, prev_lengths[prev_source], 0)
    slot_lengths = jnp.concatenate([jnp.where(own_flags == 1, 0, own_lengths), incoming_lengths])
    slot_ends = jnp.cumsum(slot_lengths)
    slot_starts = slot_ends - slot_lengths
    position = jnp.arange(TOK_CAP)
    slot_of = jnp.sum((slot_ends[None, :] <= position[:, None]).astype(jnp.int32), axis=1)
    slot_of = jnp.minimum(slot_of, slot_lengths.shape[0] - 1)
    offset = jnp.clip(position - slot_starts[slot_of], 0, context - 1)
    stacked = jnp.concatenate([captions, incoming], axis=0).reshape(-1, model_width)
    token_rows = jnp.take(stacked, slot_of * context + offset, axis=0)
    encoded = encode(token_rows, slot_starts, slot_lengths, weight_set)
    returned = from_behind(encoded[caption_count:], "dp", -1)
    own_text = jnp.where(
        (own_flags == 1)[:, None], returned[jnp.clip(before, 0, HAND - 1)], encoded[:caption_count]
    )
    text_unit = unit_rows(own_text).astype(jnp.bfloat16)
    all_texts = lax.all_gather(text_unit, "dp", axis=0, tiled=True)
    row_scores = LOGIT_SCALE * contract_last(image_unit, all_texts)
    column_scores = LOGIT_SCALE * contract_last(all_images, text_unit)
    row_peak = jnp.max(row_scores, axis=1, keepdims=True)
    row_logsum = row_peak[:, 0] + jnp.log(jnp.sum(jnp.exp(row_scores - row_peak), axis=1))
    column_peak = jnp.max(column_scores, axis=0, keepdims=True)
    column_logsum = column_peak[0] + jnp.log(jnp.sum(jnp.exp(column_scores - column_peak), axis=0))
    row_weights = jnp.exp(row_scores - row_logsum[:, None]).astype(jnp.bfloat16)
    column_weights = jnp.exp(column_scores - column_logsum[None, :]).astype(jnp.bfloat16)
    half_scale = 0.5 * LOGIT_SCALE
    image_unit_grad = half_scale * jnp.dot(
        row_weights, all_texts, preferred_element_type=jnp.float32
    )
    image_unit_grad = image_unit_grad - LOGIT_SCALE * text_unit.astype(jnp.float32)
    text_unit_grad = half_scale * contract_first(column_weights, all_images)
    text_unit_grad = text_unit_grad - LOGIT_SCALE * image_unit.astype(jnp.float32)
    row_every, column_every = (
        lax.all_gather(row_logsum, "dp", axis=0, tiled=True),
        lax.all_gather(column_logsum, "dp", axis=0, tiled=True),
    )
    cross_rows = jnp.exp(row_scores - column_every[None, :]).astype(jnp.bfloat16)
    cross_columns = jnp.exp(column_scores - row_every[:, None]).astype(jnp.bfloat16)
    image_unit_grad = image_unit_grad + half_scale * jnp.dot(
        cross_rows, all_texts, preferred_element_type=jnp.float32
    )
    text_unit_grad = text_unit_grad + half_scale * contract_first(cross_columns, all_images)
    image_value, image_back = jax.vjp(unit_rows, images.astype(jnp.float32))
    text_value, text_back = jax.vjp(unit_rows, own_text.astype(jnp.float32))
    return (image_back(image_unit_grad)[0], text_back(text_unit_grad)[0])


def solution(mesh):
    return jax.shard_map(
        body,
        mesh=mesh,
        in_specs=(P("dp", None, None), P(), P("dp", None), P(), P(), P(), P(), P(), P()),
        out_specs=(P("dp", None), P("dp", None)),
        check_vma=False,
    )
```

profile of v0, /device:TPU:0, one launch (start us, length us, event | category | flops | bytes accessed | tf_op | source)
XLA Modules:
  0.0 240.3 jit_solution(14694527201898477411)
XLA Ops:
  7.2 1.1 fusion.63
  8.3 0.6 copy-done.18
  8.9 0.5 copy-done.13
  9.4 1.5 fusion.64
  11.0 0.8 fusion.133
  12.1 0.7 fusion.87
  13.0 3.6 %gather_fusion.1 = bf16[8,77,768]{2,0,1:T(8,128)(2,1)S(1)} fusion(bf16[32,77,768]{2,0,1:T(8,128)(2,1)} %param.9, s32[1024]{0:T(1024)S(1)} %pad_clamp_fusion.2), kind=kCustom, calls=%fused_computation.1 | custom fusion | bytes 1892384 | tf_op jit(solution)/shard_map/jit(_take)/gather | solution.py:120
  16.5 1.1 broadcast_select_fusion.1
  17.6 0.5 collective-permute-start
  18.7 0.6 gather_fusion
  19.8 0.6 fusion.136
  20.4 0.7 fusion.135
  21.1 0.7 fusion.134
  21.9 4.4 %compare_select_fusion.4 = (s32[2048,1]{0,1:T(1,128)S(1)}, s32[2048,1]{0,1:T(1,128)S(1)}) fusion(s32[]{:T(128)} %bitcast.42, s32[]{:T(128)} %bitcast.43, s32[]{:T(128)} %bitcast.44, s32[]{:T(128)} %bitcast.45, s32[]{:T(128)} %bitcast.46, s32[]{:T(128)} %bitcast.48, s32[]{:T(128)} %bitcast.47, s32[2048,1]{0,1:T(1,128)S(1)} %bitcast.100), kind=kLoop, calls=%fused_computation.175 | loop fusion | flops 30720 | bytes 24604 | tf_op jit(solution)/shard_map/gather | solution.py:130
  26.3 0.8 compare_reduce_fusion.32
  27.1 20.6 %compare_and_fusion = (pred[2048]{0:T(1024)(128)(4,1)S(1)}, s32[2048]{0:T(1024)S(1)}) fusion(s32[2048]{0:T(1024)S(1)} %convert_reduce_fusion.1, pred[2048]{0:T(1024)(128)(4,1)S(1)} %get-tuple-element.38, pred[2048]{0:T(1024)(128)(4,1)S(1)} %get-tuple-element.37, pred[2048]{0:T(1024)(128)(4,1)S(1)} %get-tuple-element.36, ...), kind=kLoop, calls=%fused_computation.187 | loop fusion | flops 90112 | bytes 94340 | tf_op jit(solution)/shard_map/jit(_take)/and | solution.py:132
  47.8 0.8 fusion.29
  48.6 2.4 pad_maximum_fusion
  51.0 3.1 %copy.24 = bf16[40,77,768]{2,1,0:T(8,128)(2,1)} copy(bf16[40,77,768]{2,0,1:T(8,128)(2,1)S(1)} %pad_maximum_fusion) | data formatting | bytes 9461760 | tf_op jit(solution)/shard_map/concatenate | solution.py:131
  54.2 6.9 %reshape.374 = bf16[3080,768]{1,0:T(8,128)(2,1)} reshape(bf16[40,77,768]{2,1,0:T(8,128)(2,1)} %copy.24) | data formatting | bytes 9461760 | tf_op jit(solution)/shard_map/reshape | solution.py:131
  61.1 13.0 %gather_fusion.2 = bf16[2048,768]{1,0:T(8,128)(2,1)} fusion(bf16[3080,768]{1,0:T(8,128)(2,1)} %reshape.374, s32[2048]{0:T(1024)S(1)} %broadcast_clamp_fusion), kind=kCustom, calls=%fused_computation.2 | custom fusion | bytes 6299648 | tf_op jit(solution)/shard_map/jit(_take)/gather | solution.py:132
  74.1 2.6 %convert_reduce_fusion = (f32[2048]{0:T(1024)S(1)}, bf16[2048,768]{1,0:T(8,128)(2,1)S(1)}) fusion(bf16[2048,768]{1,0:T(8,128)(2,1)} %gather_fusion.2, pred[2048]{0:T(1024)(128)(4,1)S(1)} %get-tuple-element.51), kind=kLoop, calls=%fused_computation.8 | loop fusion | flops 4716544 | bytes 6301696 | tf_op jit(solution)/shard_map/reduce_sum | solution.py:26
  76.8 1.7 copy-done.2
  78.5 1.1 fusion.3
  79.6 3.6 %gather_fusion.3 = bf16[40,768]{1,0:T(8,128)(2,1)} fusion(bf16[2048,768]{1,0:T(8,128)(2,1)} %copy-done.2, s32[1024]{0:T(1024)S(1)} %pad_clamp_fusion.1), kind=kCustom, calls=%fused_computation.3 | custom fusion | bytes 123040 | tf_op jit(solution)/shard_map/gather | solution.py:74
  83.2 3.6 %fusion.4 = bf16[2048,768]{1,0:T(8,128)(2,1)} fusion(bf16[2048,768]{1,0:T(8,128)(2,1)} %copy-done.2, f32[2048]{0:T(1024)S(1)} %add_rsqrt_fusion, f32[2048]{0:T(1024)S(1)} %broadcast_multiply_fusion), kind=kLoop, calls=%fused_computation.13 | loop fusion | flops 6291456 | bytes 6307840 | tf_op jit(solution)/shard_map/convert_element_type | solution.py:52
  86.8 3.7 %gather_fusion.4 = bf16[40,768]{1,0:T(8,128)(2,1)} fusion(bf16[2048,768]{1,0:T(8,128)(2,1)} %fusion.4, s32[1024]{0:T(1024)} %copy-done.12), kind=kCustom, calls=%fused_computation.4 | custom fusion | bytes 123040 | tf_op jit(solution)/shard_map/gather | solution.py:55
  90.5 1.8 convolution_convert_fusion.2
  92.3 1.0 reshape.376
  93.3 7.5 %convolution_convert_fusion = bf16[2048,1536]{0,1:T(8,128)(2,1)S(1)} fusion(bf16[2048,768]{1,0:T(8,128)(2,1)} %fusion.4, bf16[768,1536]{1,0:T(8,128)(2,1)S(1)} %copy-done), kind=kOutput, calls=%fused_computation.9 | convolution fusion | flops 4834983936 | bytes 11796480 | tf_op jit(solution)/shard_map/dot_general | solution.py:53
  100.8 3.2 %fusion.132 = (bf16[2048,768]{0,1:T(8,128)(2,1)}, bf16[2048,768]{0,1:T(8,128)(2,1)}) fusion(bf16[2048,1536]{0,1:T(8,128)(2,1)S(1)} %convolution_convert_fusion), kind=kLoop, calls=%fused_computation.268 | loop fusion | bytes 12582912 | tf_op jit(solution)/shard_map/slice | solution.py:58
  104.0 5.3 %fusion.137 = (f32[12,40]{1,0:T(8,128)S(1)}, f32[12,40,2048]{2,1,0:T(8,128)}) fusion(pred[40,2048]{1,0:T(8,128)(4,1)S(1)} %copy-done.11, bf16[2048,12,64]{0,2,1:T(8,128)(2,1)} %bitcast.99, bf16[40,12,64]{2,1,0:T(8,128)(2,1)S(1)} %reshape.376), kind=kOutput, calls=%fused_computation.273 | convolution fusion | flops 129763328 | bytes 7223168 | tf_op jit(solution)/shard_map/sub | solution.py:68
  109.3 4.2 %fusion.11 = bf16[40,12,64]{2,0,1:T(8,128)(2,1)S(1)} fusion(bf16[2048,12,64]{0,2,1:T(8,128)(2,1)} %bitcast.98, f32[12,40,2048]{2,1,0:T(8,128)} %get-tuple-element.103, f32[12,40]{1,0:T(8,128)S(1)} %get-tuple-element.102), kind=kOutput, calls=%fused_computation.27 | convolution fusion | flops 127825920 | bytes 7141248 | tf_op jit(solution)/shard_map/hsr,rhd->shd/dot_general | solution.py:70
  114.4 6.3 %fusion.141 = (f32[40]{0:T(128)S(1)}, f32[40,768]{1,0:T(8,128)S(1)}) fusion(f32[40,768]{1,0:T(8,128)S(1)} %get-tuple-element.105, bf16[3072,768]{1,0:T(8,128)(2,1)} %param.16, bf16[768,3072]{1,0:T(8,128)(2,1)} %param.15, f32[40]{0:T(128)S(1)} %add_rsqrt_fusion.2, f32[40]{0:T(128)S(1)} %broadcast_multiply_fusion.2), kind=kOutput, calls=%fused_computation.275 | convolution fusion | flops 385628128 | bytes 9683424 | tf_op jit(solution)/shard_map/dot_general | solution.py:83
  121.3 6.0 %collective-permute-start.1 = (bf16[8,768]{1,0:T(8,128)(2,1)S(1)}, bf16[8,768]{1,0:T(8,128)(2,1)S(1)}, u32[]{:S(2)}, u32[]{:S(2)}) collective-permute-start(bf16[8,768]{1,0:T(8,128)(2,1)S(1)} %slice.81), channel_id=1, source_target_pairs={{0,31},{1,0},{2,1},{3,2},{4,3},{5,4},{6,5},{7,6},{8,7},{9,8},{10,9... | collective-permute-start | bytes 36872 | tf_op jit(solution)/shard_map/ppermute | solution.py:21
  127.3 1.4 collective-permute-done.1
  128.7 0.6 gather_fusion.5
  129.5 0.7 fusion.67
  130.3 2.1 fusion.143
  132.7 1.8 fusion.13
  134.6 51.8 %all-gather.3.cloned.1.call-done = bf16[1024,768]{1,0:T(8,128)(2,1)} async-done(((bf16[32,768]{1,0:T(8,128)(2,1)}), bf16[1024,768]{1,0:T(8,128)(2,1)}) %all-gather.3.cloned.1.call-update) | async-done | bytes 1572880 | tf_op jit(solution)/shard_map/all_gather | solution.py:139
  186.4 2.1 fusion.142
  188.8 38.9 %all-reduce.2 = (f32[1024]{0:T(1024)S(1)}, f32[1024]{0:T(1024)S(1)}) all-reduce(f32[1024]{0:T(1024)S(1)} %get-tuple-element.43, f32[1024]{0:T(1024)S(1)} %get-tuple-element.41), channel_id=1, replica_groups=mesh['dp'=32] {'dp'}, use_global_device_ids=true, to_apply=%add | all-reduce | flops 2048 | bytes 16384
  227.7 1.9 fusion.15
  229.6 1.9 fusion.65
  231.6 0.5 fusion.68
  232.1 0.7 add_add_fusion.1
  232.8 0.7 add_add_fusion
  (96 shorter events, 4.1 us)
Async XLA Ops:
  7.2 86.1 %copy-start = (bf16[768,1536]{1,0:T(8,128)(2,1)S(1)}, bf16[768,1536]{1,0:T(8,128)(2,1)}, u32[]{:S(2)}) copy-start(bf16[768,1536]{1,0:T(8,128)(2,1)} %param.13) | copy-start | bytes 7077892
  7.2 123.1 %all-gather.5.cloned.1.call-start = ((), (), s32[]{:S(2)}) async-start(), calls=%async_computation.1 | async-start | bytes 1622016 | tf_op jit(solution)/shard_map/all_gather | solution.py:108
  8.3 0.6 copy-start.18
  8.9 0.5 copy-start.13
  10.9 175.5 %all-gather.3.cloned.1.call-start = ((), (), s32[]{:S(2)}) async-start(), calls=%async_computation | async-start | bytes 1622016 | tf_op jit(solution)/shard_map/all_gather | solution.py:139
  11.9 1.0 copy-start.15
  17.6 31.0 %collective-permute-start = (bf16[8,77,768]{2,0,1:T(8,128)(2,1)}, bf16[8,77,768]{2,0,1:T(8,128)(2,1)S(1)}, u32[]{:S(2)}, u32[]{:S(2)}) collective-permute-start(bf16[8,77,768]{2,0,1:T(8,128)(2,1)} %broadcast_select_fusion.1), channel_id=1, source_target_pairs={{0,1},{1,2},{2,3},{3,4},{4,5},{5,6},{6,7},{7,8},{8,9},{9,10},{10,1... | collective-permute-start | bytes 2838536 | tf_op jit(solution)/shard_map/ppermute | solution.py:21
  47.8 31.8 %copy-start.12 = (s32[1024]{0:T(1024)}, s32[1024]{0:T(1024)S(1)}, u32[]{:S(2)}) copy-start(s32[1024]{0:T(1024)S(1)} %pad_clamp_fusion.1) | copy-start | bytes 12292
  76.8 1.7 copy-start.2
  83.2 7.3 %copy-start.4 = (bf16[768,768]{1,0:T(8,128)(2,1)S(1)}, bf16[768,768]{1,0:T(8,128)(2,1)}, u32[]{:S(2)}) copy-start(bf16[768,768]{1,0:T(8,128)(2,1)} %param.12) | copy-start | bytes 3538948
  100.8 3.2 %copy-start.11 = (pred[40,2048]{1,0:T(8,128)(4,1)S(1)}, pred[40,2048]{1,0:T(8,128)(4,1)}, u32[]{:S(2)}) copy-start(pred[40,2048]{1,0:T(8,128)(4,1)} %fusion.29) | copy-start | bytes 245764
  109.3 4.4 %copy-start.6 = (bf16[768,768]{1,0:T(8,128)(2,1)S(1)}, bf16[768,768]{1,0:T(8,128)(2,1)}, u32[]{:S(2)}) copy-start(bf16[768,768]{1,0:T(8,128)(2,1)} %param.14) | copy-start | bytes 3538948
  109.3 4.4 %copy-start.10 = (bf16[40,768]{1,0:T(8,128)(2,1)S(1)}, bf16[40,768]{1,0:T(8,128)(2,1)}, u32[]{:S(2)}) copy-start(bf16[40,768]{1,0:T(8,128)(2,1)} %gather_fusion.3) | copy-start | bytes 184324
  114.3 6.6 %copy-start.5 = (bf16[768,768]{1,0:T(8,128)(2,1)S(1)}, bf16[768,768]{1,0:T(8,128)(2,1)}, u32[]{:S(2)}) copy-start(bf16[768,768]{1,0:T(8,128)(2,1)} %param.17) | copy-start | bytes 3538948
  114.3 12.9 %copy-start.17 = (s32[32]{0:T(128)S(1)}, s32[32]{0:T(128)}, u32[]{:S(2)}) copy-start(s32[32]{0:T(128)} %get-tuple-element.4) | copy-start | bytes 388
  114.4 15.0 %copy-start.16 = (pred[32]{0:T(512)(128)(4,1)S(1)}, pred[32]{0:T(512)(128)(4,1)}, u32[]{:S(2)}) copy-start(pred[32]{0:T(512)(128)(4,1)} %copy-done.15) | copy-start | bytes 100
  120.7 12.0 %copy-start.7 = (bf16[32,768]{1,0:T(8,128)(2,1)S(1)}, bf16[32,768]{1,0:T(8,128)(2,1)}, u32[]{:S(2)}) copy-start(bf16[32,768]{1,0:T(8,128)(2,1)} %fusion.64) | copy-start | bytes 147460
  121.3 7.4 %collective-permute-start.1 = (bf16[8,768]{1,0:T(8,128)(2,1)S(1)}, bf16[8,768]{1,0:T(8,128)(2,1)S(1)}, u32[]{:S(2)}, u32[]{:S(2)}) collective-permute-start(bf16[8,768]{1,0:T(8,128)(2,1)S(1)} %slice.81), channel_id=1, source_target_pairs={{0,31},{1,0},{2,1},{3,2},{4,3},{5,4},{6,5},{7,6},{8,7},{9,8},{10,9... | collective-permute-start | bytes 36872 | tf_op jit(solution)/shard_map/ppermute | solution.py:21
  130.2 97.4 %copy-start.8 = (bf16[32,768]{1,0:T(8,128)(2,1)S(1)}, bf16[32,768]{1,0:T(8,128)(2,1)}, u32[]{:S(2)}) copy-start(bf16[32,768]{1,0:T(8,128)(2,1)} %fusion.67) | copy-start | bytes 147460
  132.4 97.2 %copy-start.9 = (bf16[32,768]{1,0:T(8,128)(2,1)S(1)}, bf16[32,768]{1,0:T(8,128)(2,1)}, u32[]{:S(2)}) copy-start(bf16[32,768]{1,0:T(8,128)(2,1)} %param.11) | copy-start | bytes 147460
  134.6 96.9 %copy-start.19 = (f32[32]{0:T(128)S(1)}, f32[32]{0:T(128)}, u32[]{:S(2)}) copy-start(f32[32]{0:T(128)} %copy-done.18) | copy-start | bytes 388
  188.5 43.6 %copy-start.14 = (f32[32]{0:T(128)S(1)}, f32[32]{0:T(128)}, u32[]{:S(2)}) copy-start(f32[32]{0:T(128)} %copy-done.13) | copy-start | bytes 388
  188.5 45.0 %copy-start.1 = (bf16[768,1536]{1,0:T(8,128)(2,1)S(1)}, bf16[768,1536]{1,0:T(8,128)(2,1)}, u32[]{:S(2)}) copy-start(bf16[768,1536]{1,0:T(8,128)(2,1)} %param.13) | copy-start | bytes 7077892
  227.7 3.9 %copy-start.3 = (bf16[1024,768]{1,0:T(8,128)(2,1)S(1)}, bf16[1024,768]{1,0:T(8,128)(2,1)}, u32[]{:S(2)}) copy-start(bf16[1024,768]{1,0:T(8,128)(2,1)} %all-gather.5.cloned.1.call-done) | copy-start | bytes 4718596
Sparse Core Ops, SparseCore 0:
  11.0 59.7 all-gather.4
  130.4 55.9 all-gather.2
where the time goes:
time: 242 us; the launch traced here: 240 us
  waiting for transfers between devices  53.2 us (22%)
  local copies, waits for them, and re-layouts  45.6 us (19%)
  other arithmetic  45.4 us (19%)
  blocking collectives  38.9 us (16%)
  matrix products  36.2 us (15%)
  between operations  14.5 us (6%)
  starting transfers between devices  6.53 us (3%)
    all_gather x1, waiting for transfers between devices, body(): all_texts = lax.all_gather(text_unit, 'dp', axis=0, tiled=True)  51.8 us
    unnamed x1, blocking collectives  38.9 us
    and x1, other arithmetic, body(): token_rows = jnp.take(stacked, slot_of * context + offset, axis=0)  20.6 us
    gather x1, local copies, waits for them, and re-layouts, body(): token_rows = jnp.take(stacked, slot_of * context + offset, axis=0)  13 us
    dot_general x1, matrix products, encode(): jnp.dot(normed, w_keyval, preferred_element_type=jnp.float32)  7.47 us
    reshape x1, local copies, waits for them, and re-layouts, body(): jnp.concatenate([captions, incoming], axis=0).reshape(-1, model_width)  6.92 us
    ppermute x2, starting transfers between devices, from_behind(): return lax.ppermute(value, axis, pairs)  6.45 us
    dot_general x1, matrix products, encode(): jnp.dot(hidden, w_down, preferred_element_type=jnp.float32)  6.34 us
  transfers between devices with their start and end apart: 4, of which 2 were waited for; matrix products, arithmetic and copies ran while one was open for 47% of the time, Pallas kernels for 0%

commit v1 on v0

v1 whole, which is shorter than its diff:
```python
import functools
import math

import jax
import jax.numpy as jnp
from jax import lax
from jax.experimental import pallas as pl
from jax.experimental.pallas import tpu as pltpu
from jax.sharding import PartitionSpec as P

HEADS = 12
HEAD_ROWS = 16
LOGIT_SCALE = 100.0
EPS_NORM = 1e-05
EPS_UNIT = 1e-06
BF16 = jnp.bfloat16
F32 = jnp.float32
VMEM_LIMIT = 60 * 1024 * 1024


def layer_norm(values):
    center = values - jnp.mean(values, axis=-1, keepdims=True)
    spread = jnp.mean(center * center, axis=-1, keepdims=True)
    return center * lax.rsqrt(spread + EPS_NORM)


def inverse_norm(values):
    return lax.rsqrt(jnp.sum(values * values, axis=-1, keepdims=True) + EPS_UNIT)


def dot(left, right):
    return jnp.dot(left, right, preferred_element_type=F32)


def dot_last(left, right):
    return lax.dot_general(left, right, (((1,), (1,)), ((), ())), preferred_element_type=F32)


def erf(x):
    x = jnp.clip(x, -3.832506856900711, 3.832506856900711)
    y = x * x
    top = jnp.full_like(x, 0.00022905065861350646)
    for c in (
        0.0034082910107109506,
        0.050955695062380861,
        0.18520832239976145,
        1.128379143519084,
    ):
        top = top * y + c
    bottom = jnp.full_like(x, -1.1791602954361697e-7)
    for c in (
        0.000023547966471313185,
        0.0010179625278914885,
        0.014070470171167667,
        0.11098505178285362,
        0.49746925110067538,
        1.0,
    ):
        bottom = bottom * y + c
    return x * top / bottom


def encode_kernel(
    layout_ref, captions_ref, *refs, chunk
):
    (weight_refs, (embed_ref, unit_ref)) = (refs[:6], refs[6:8])
    (caps, normed, last, mapped, score, mix) = refs[8:14]
    weights, cap_sem, weight_sem = refs[14:20], refs[20], refs[21]
    count, context, width = caps.shape
    head_dim = width // HEADS
    base = lax.axis_index("dp") * count

    def cap_copy(i):
        part = pl.ds(i * chunk, chunk)
        return pltpu.make_async_copy(captions_ref.at[part], caps.at[part], cap_sem.at[i])

    def weight_copy(i):
        return pltpu.make_async_copy(weight_refs[i], weights[i], weight_sem.at[i])

    for i in range(count // chunk):
        cap_copy(i).start()
    for i in range(6):
        weight_copy(i).start()
    w_query, w_keyval, w_out, w_up, w_down, w_proj = weights

    row = lax.broadcasted_iota(jnp.int32, (context, width), 0)
    for i in range(count // chunk):
        cap_copy(i).wait()

        def normalise(c, _):
            value = caps[c].astype(F32)
            normed[c] = layer_norm(value).astype(BF16)
            picked = jnp.where(row == layout_ref[0, base + c] - 1, value, 0.0)
            last[pl.ds(c, 1), :] = jnp.sum(picked, axis=0, keepdims=True)
            return _

        lax.fori_loop(i * chunk, (i + 1) * chunk, normalise, 0, unroll=2)

    tokens = last[...]
    weight_copy(0).wait()
    query = dot(layer_norm(tokens).astype(BF16), w_query[...]).astype(BF16).astype(F32)
    shape = (count, HEAD_ROWS, width)
    own_head = (
        lax.broadcasted_iota(jnp.int32, shape, 2) // head_dim
        == lax.broadcasted_iota(jnp.int32, shape, 1)
    )
    spread = jnp.where(own_head, jnp.broadcast_to(query[:, None, :], shape), 0.0)
    spread = spread.reshape(count * HEAD_ROWS, width).astype(BF16)
    weight_copy(1).wait()
    mapped[...] = dot_last(spread, w_keyval[:, :width]).astype(BF16).reshape(shape)

    for c in range(count):
        score[c, :, :context] = dot_last(mapped[c], normed[c])
    position = lax.broadcasted_iota(jnp.int32, (HEAD_ROWS, score.shape[2]), 1)
    scale = 1.0 / math.sqrt(head_dim)
    for c in range(count):
        masked = jnp.where(position < layout_ref[0, base + c], score[c] * scale, -jnp.inf)
        exponent = jnp.exp(masked - jnp.max(masked, axis=-1, keepdims=True))
        attention = exponent / jnp.sum(exponent, axis=-1, keepdims=True)
        score[c] = attention
    for c in range(count):
        mix[c] = dot(score[c, :, :context].astype(BF16), normed[c]).astype(BF16)
    mixed = dot(mix[...].reshape(count * HEAD_ROWS, width), w_keyval[:, width:]).reshape(shape)
    mixed = jnp.sum(jnp.where(own_head, mixed, 0.0), axis=1).astype(BF16)
    weight_copy(2).wait()
    residual = (tokens + dot(mixed, w_out[...])).astype(BF16).astype(F32)
    inner = layer_norm(residual).astype(BF16)
    weight_copy(3).wait()
    hidden = dot(inner, w_up[...])
    hidden = (0.5 * hidden * (1.0 + erf(hidden * math.sqrt(0.5)))).astype(BF16)
    weight_copy(4).wait()
    final = residual + dot(hidden, w_down[...])
    pooled = layer_norm(final).astype(BF16)
    weight_copy(5).wait()
    embed = dot(pooled, w_proj[...]).astype(BF16)
    embed_ref[...] = embed
    embed = embed.astype(F32)
    unit_ref[...] = (embed * inverse_norm(embed)).astype(BF16)


def encode(layout, captions, weights):
    count, context, width = captions.shape
    chunk = 4 if count % 4 == 0 else 1
    joint = weights[5].shape[1]
    result = jax.ShapeDtypeStruct((count, joint), BF16)
    flops = 2 * count * (sum(w.size for w in weights) + 2 * HEAD_ROWS * context * width)
    return pl.pallas_call(
        functools.partial(encode_kernel, chunk=chunk),
        out_shape=(result, result),
        in_specs=[pl.BlockSpec(memory_space=pltpu.SMEM)]
        + [pl.BlockSpec(memory_space=pl.ANY)] * 7,
        out_specs=(pl.BlockSpec(memory_space=pltpu.VMEM),) * 2,
        scratch_shapes=[
            pltpu.VMEM((count, context, width), BF16),
            pltpu.VMEM((count, context, width), BF16),
            pltpu.VMEM((count, width), F32),
            pltpu.VMEM((count, HEAD_ROWS, width), BF16),
            pltpu.VMEM((count, HEAD_ROWS, 128), F32),
            pltpu.VMEM((count, HEAD_ROWS, width), BF16),
        ]
        + [pltpu.VMEM(w.shape, w.dtype) for w in weights]
        + [
            pltpu.SemaphoreType.DMA((count // chunk,)),
            pltpu.SemaphoreType.DMA((6,)),
        ],
        compiler_params=pltpu.CompilerParams(vmem_limit_bytes=VMEM_LIMIT),
        cost_estimate=pl.CostEstimate(
            flops=flops,
            bytes_accessed=2 * (captions.size + sum(w.size for w in weights)),
            transcendentals=count * HEAD_ROWS * 128,
        ),
        name="encode",
    )(layout, captions, *weights)


def unit_grad(grad, value):
    inverse = inverse_norm(value)
    inner = jnp.sum(value * grad, axis=-1, keepdims=True)
    return grad * inverse - value * (inner * inverse * inverse * inverse)


def loss_kernel(images_a, images_b, texts_a, texts_b, embed, image_out, text_out, *scratch, tile):
    unit, sides, row_lse, own_rows = scratch
    half = images_a.shape[0]
    count = embed.shape[0]
    total = 2 * half
    texts = (texts_a, texts_b)
    for h, part in enumerate((images_a, images_b)):

        def normalise(i, _, part=part, h=h):
            value = part[pl.ds(i * tile, tile), :].astype(F32)
            unit[pl.ds(h * half + i * tile, tile), :] = (value * inverse_norm(value)).astype(BF16)
            return _

        lax.fori_loop(0, half // tile, normalise, 0)

    def scores(rows):
        return [LOGIT_SCALE * dot_last(rows, t[...]) for t in texts]

    def step(i, carry):
        rows = pl.ds(i * tile, tile)
        both = scores(unit[rows, :])
        sides[rows, :] = both[0][:, :128]
        peak = jnp.maximum(
            jnp.max(both[0], axis=1, keepdims=True), jnp.max(both[1], axis=1, keepdims=True)
        )
        total_row = jnp.zeros((tile, 1), F32)
        result = []
        for s, (top, mass) in zip(both, carry):
            total_row += jnp.sum(jnp.exp(s - peak), axis=1, keepdims=True)
            higher = jnp.maximum(top, jnp.max(s, axis=0, keepdims=True))
            mass = mass * jnp.exp(top - higher) + jnp.sum(
                jnp.exp(s - higher), axis=0, keepdims=True
            )
            result.append((higher, mass))
        row_lse[rows, :] = jnp.broadcast_to(peak + jnp.log(total_row), (tile, 128))
        return tuple(result)

    start = (jnp.full((1, half), -jnp.inf, F32), jnp.zeros((1, half), F32))
    ends = lax.fori_loop(0, total // tile, step, (start, start))
    column_lse = [top + jnp.log(mass) for top, mass in ends]

    own_unit = unit[:count, :]
    own_row_lse = row_lse[:count, :1]
    grad = -LOGIT_SCALE * texts_a[:count, :].astype(F32)
    for s, lse, t in zip(scores(own_unit), column_lse, texts):
        weights = jnp.concatenate(
            [jnp.exp(s - own_row_lse).astype(BF16), jnp.exp(s - lse).astype(BF16)], axis=0
        )
        both = dot(weights, t[...])
        grad += (0.5 * LOGIT_SCALE) * (both[:count] + both[count:])
    image_out[...] = unit_grad(grad, images_a[:count, :].astype(F32))

    side = sides[...]
    grad = -LOGIT_SCALE * own_unit.astype(F32)
    by_row = jnp.exp(side - row_lse[...]).T[:count].astype(BF16)
    by_column = jnp.exp(side - column_lse[0][:, :128]).T[:count].astype(BF16)
    both = dot(jnp.concatenate([by_row, by_column], axis=0), unit[...])
    grad += (0.5 * LOGIT_SCALE) * (both[:count] + both[count:])
    text_out[...] = unit_grad(grad, embed[...].astype(F32))


def loss(images, texts, embed):
    half, width = images[0].shape
    count = embed.shape[0]
    tile = 128
    result = jax.ShapeDtypeStruct((count, width), F32)
    return pl.pallas_call(
        functools.partial(loss_kernel, tile=tile),
        out_shape=(result, result),
        in_specs=[pl.BlockSpec(memory_space=pltpu.VMEM)] * 5,
        out_specs=(pl.BlockSpec(memory_space=pltpu.VMEM),) * 2,
        scratch_shapes=[
            pltpu.VMEM((2 * half, width), BF16),
            pltpu.VMEM((2 * half, 128), F32),
            pltpu.VMEM((2 * half, 128), F32),
            pltpu.VMEM((8, 128), F32),
        ],
        compiler_params=pltpu.CompilerParams(vmem_limit_bytes=48 * 1024 * 1024),
        cost_estimate=pl.CostEstimate(
            flops=8 * half * half * width, bytes_accessed=8 * half * width, transcendentals=8 * half * half
        ),
        name="loss",
    )(*images, *texts, embed)


def from_partner(value, mask):
    devices = lax.axis_size("dp")
    return lax.ppermute(value, "dp", [(i, i ^ mask) for i in range(devices)])


def digit_masks(devices):
    groups, high = [], devices
    while high > 2:
        low = max(high // 4, 2)
        groups.append([k * low for k in range(1, high // low)])
        high = low
    return groups


def gather_rail(value):
    for masks in digit_masks(lax.axis_size("dp")):
        value = jnp.concatenate([value] + [from_partner(value, m) for m in masks], axis=0)
    return value


def body(captions, layout, images, *weights):
    image_rail = gather_rail(images)
    image_other = from_partner(image_rail, 1)
    embed, unit = encode(layout, captions, weights)
    text_rail = gather_rail(unit)
    text_other = from_partner(text_rail, 1)
    return loss((image_rail, image_other), (text_rail, text_other), embed)


def solution(mesh):
    return jax.shard_map(
        body,
        mesh=mesh,
        in_specs=(P("dp", None, None), P(), P("dp", None), P(), P(), P(), P(), P(), P()),
        out_specs=(P("dp", None), P("dp", None)),
        check_vma=False,
    )
```

time: 242 us -> 66.9 us (0.28)
  other arithmetic: 45.4 us -> 0 us
  waiting for transfers between devices: 53.2 us -> 13.4 us
  blocking collectives: 38.9 us -> 0 us
  local copies, waits for them, and re-layouts: 45.6 us -> 7.78 us
  matrix products: 36.2 us -> 0 us
  Pallas kernels: 0 us -> 25.6 us
  between operations: 14.5 us -> 0.77 us
  starting transfers between devices: 6.53 us -> 19.1 us
    all_gather x2 -> x0, waiting for transfers between devices: 51.8 us -> none  [the longest x1 51.8 us: body(): all_texts = lax.all_gather(text_unit, 'dp', axis=0, tiled=True)]
    unnamed x1 -> x0, blocking collectives: 38.9 us -> none
    dot_general x12 -> x0, matrix products: 30.9 us -> none  [the longest x1 7.47 us: encode(): jnp.dot(normed, w_keyval, preferred_element_type=jnp.float32)]
    gather x9 -> x0, local copies, waits for them, and re-layouts: 27.2 us -> none  [the longest x1 13 us: body(): token_rows = jnp.take(stacked, slot_of * context + offset, axis=0)]
    pallas_call x0 -> x2, Pallas kernels: none -> 25.6 us  [the longest x1 15.7 us: encode(): pl.pallas_call(functools.partial(encode_kernel, chunk=chunk), out_shape=(...]
    and x3 -> x0, other arithmetic: 20.7 us -> none  [the longest x1 20.6 us: body(): token_rows = jnp.take(stacked, slot_of * context + offset, axis=0)]
    ppermute x2 -> x14, starting transfers between devices: 6.45 us -> 19.1 us  [from_partner(): return lax.ppermute(value, 'dp', [(i, i ^ mask) for i in range(devices)])]
    ppermute x2 -> x14, waiting for transfers between devices: 1.4 us -> 13.4 us  [from_partner(): return lax.ppermute(value, 'dp', [(i, i ^ mask) for i in range(devices)])]
  transfers between devices with their start and end apart: 4 -> 14, of which waited for: 2 -> 7; matrix products, arithmetic and copies ran while one was open for 47% -> 1% of each run, Pallas kernels for 0% -> 0%
where the time goes in v1:
time: 66.9 us; the launch traced here: 66.6 us
  Pallas kernels  25.6 us (38%)
  starting transfers between devices  19.1 us (29%)
  waiting for transfers between devices  13.4 us (20%)
  local copies, waits for them, and re-layouts  7.78 us (12%)
  between operations  0.77 us (1%)
    ppermute x14, starting transfers between devices, from_partner(): return lax.ppermute(value, 'dp', [(i, i ^ mask) for i in range(devices)])  19.1 us
    pallas_call x1, Pallas kernels, encode(): pl.pallas_call(functools.partial(encode_kernel, chunk=chunk), out_shape=(...  15.7 us
    ppermute x14, waiting for transfers between devices, from_partner(): return lax.ppermute(value, 'dp', [(i, i ^ mask) for i in range(devices)])  13.4 us
    pallas_call x1, Pallas kernels, loss(): pl.pallas_call(functools.partial(loss_kernel, tile=tile), out_shape=(resu...  9.92 us
    unnamed x15, local copies, waits for them, and re-layouts  7.73 us
  transfers between devices with their start and end apart: 14, of which 7 were waited for; matrix products, arithmetic and copies ran while one was open for 1% of the time, Pallas kernels for 0%

profile of v1, /device:TPU:0, one launch (start us, length us, event | category | flops | bytes accessed | tf_op | source)
XLA Modules:
  0.0 66.6 jit_solution(5468219350472111959)
XLA Ops:
  0.6 6.0 %copy.11.captions_ref = bf16[32,77,768]{2,1,0:T(8,128)(2,1)} copy(bf16[32,77,768]{2,0,1:T(8,128)(2,1)} %param.9) | data formatting | bytes 7569408 | tf_op args[0]
  6.7 0.0 copy-start.1
  6.7 15.7 %encode.1 = (bf16[32,768]{1,0:T(8,128)(2,1)}, bf16[32,768]{1,0:T(8,128)(2,1)}) custom-call(s32[2,1024]{1,0:T(2,128)} %layout_ref.1, bf16[32,77,768]{2,1,0:T(8,128)(2,1)} %copy.11.captions_ref, bf16[768,768]{1,0:T(8,128)(2,1)} %refs_0_.1, bf16[768,1536]{1,0:T(8,128)(2,1)} %refs_1_.1, bf16[768,768]{1,0:T(8,128)(2,1)} %refs_2_.1, bf16[768,3072]{1,0:T(8,128)(2,1)} %refs_3_.1, ...), custom_call_target="tpu_custom_call" | custom-call | flops 611844096 | bytes 19120128 | tf_op jit(solution)/shard_map/encode/pallas_call | solution.py:147
  22.4 3.1 %collective-permute-start.7 = (bf16[32,768]{1,0:T(8,128)(2,1)}, bf16[32,768]{1,0:T(8,128)(2,1)S(1)}, u32[]{:S(2)}, u32[]{:S(2)}) collective-permute-start(bf16[32,768]{1,0:T(8,128)(2,1)} %get-tuple-element.4), channel_id=1, source_target_pairs={{0,8},{1,9},{2,10},{3,11},{4,12},{5,13},{6,14},{7,15},{8,0},{9,1},... | collective-permute-start | bytes 147464 | tf_op jit(solution)/shard_map/ppermute | solution.py:269
  25.5 2.6 %collective-permute-start.8 = (bf16[32,768]{1,0:T(8,128)(2,1)}, bf16[32,768]{1,0:T(8,128)(2,1)S(1)}, u32[]{:S(2)}, u32[]{:S(2)}) collective-permute-start(bf16[32,768]{1,0:T(8,128)(2,1)} %get-tuple-element.4), channel_id=1, source_target_pairs={{0,16},{1,17},{2,18},{3,19},{4,20},{5,21},{6,22},{7,23},{8,24},{9,... | collective-permute-start | bytes 147464 | tf_op jit(solution)/shard_map/ppermute | solution.py:269
  28.1 0.0 collective-permute-start.9
  28.1 0.0 copy-done.1
  28.1 0.9 %collective-permute-start = (bf16[32,768]{1,0:T(8,128)(2,1)S(1)}, bf16[32,768]{1,0:T(8,128)(2,1)S(1)}, u32[]{:S(2)}, u32[]{:S(2)}) collective-permute-start(bf16[32,768]{1,0:T(8,128)(2,1)S(1)} %copy-done.1), channel_id=1, source_target_pairs={{0,8},{1,9},{2,10},{3,11},{4,12},{5,13},{6,14},{7,15},{8,0},{9,1},... | collective-permute-start | bytes 147464 | tf_op jit(solution)/shard_map/ppermute | solution.py:269
  29.0 3.5 %collective-permute-start.1 = (bf16[32,768]{1,0:T(8,128)(2,1)S(1)}, bf16[32,768]{1,0:T(8,128)(2,1)S(1)}, u32[]{:S(2)}, u32[]{:S(2)}) collective-permute-start(bf16[32,768]{1,0:T(8,128)(2,1)S(1)} %copy-done.1), channel_id=1, source_target_pairs={{0,16},{1,17},{2,18},{3,19},{4,20},{5,21},{6,22},{7,23},{8,24},{9,... | collective-permute-start | bytes 147464 | tf_op jit(solution)/shard_map/ppermute | solution.py:269
  32.5 0.8 %constant_dynamic-update-slice_fusion.14 = (bf16[128,768]{1,0:T(8,128)(2,1)S(1)}, bf16[512,768]{1,0:T(8,128)(2,1)S(1)}) fusion(bf16[32,768]{1,0:T(8,128)(2,1)} %get-tuple-element.4), kind=kLoop, calls=%fused_computation.14 | loop fusion | bytes 147456
  33.3 0.0 collective-permute-done.7
  33.3 0.1 collective-permute-start.2
  33.4 0.0 collective-permute-done.8
  33.4 0.8 %collective-permute-done.9 = bf16[32,768]{1,0:T(8,128)(2,1)S(1)} collective-permute-done((bf16[32,768]{1,0:T(8,128)(2,1)}, bf16[32,768]{1,0:T(8,128)(2,1)S(1)}, u32[]{:S(2)}, u32[]{:S(2)}) %collective-permute-start.9) | collective-permute-done | bytes 49184 | tf_op jit(solution)/shard_map/ppermute | solution.py:269
  34.2 1.6 %collective-permute-start.10 = (bf16[128,768]{1,0:T(8,128)(2,1)S(1)}, bf16[128,768]{1,0:T(8,128)(2,1)S(1)}, u32[]{:S(2)}, u32[]{:S(2)}) collective-permute-start(bf16[128,768]{1,0:T(8,128)(2,1)S(1)} %get-tuple-element.6), channel_id=1, source_target_pairs={{0,2},{1,3},{2,0},{3,1},{4,6},{5,7},{6,4},{7,5},{8,10},{9,11},{10,... | collective-permute-start | bytes 589832 | tf_op jit(solution)/shard_map/ppermute | solution.py:269
  35.7 1.5 %collective-permute-start.11 = (bf16[128,768]{1,0:T(8,128)(2,1)S(1)}, bf16[128,768]{1,0:T(8,128)(2,1)S(1)}, u32[]{:S(2)}, u32[]{:S(2)}) collective-permute-start(bf16[128,768]{1,0:T(8,128)(2,1)S(1)} %get-tuple-element.6), channel_id=1, source_target_pairs={{0,4},{1,5},{2,6},{3,7},{4,0},{5,1},{6,2},{7,3},{8,12},{9,13},{10,... | collective-permute-start | bytes 589832 | tf_op jit(solution)/shard_map/ppermute | solution.py:269
  37.3 0.0 collective-permute-done
  37.3 0.5 collective-permute-start.12
  37.8 0.0 collective-permute-done.1
  37.8 1.5 %collective-permute-done.2 = bf16[32,768]{1,0:T(8,128)(2,1)S(1)} collective-permute-done((bf16[32,768]{1,0:T(8,128)(2,1)S(1)}, bf16[32,768]{1,0:T(8,128)(2,1)S(1)}, u32[]{:S(2)}, u32[]{:S(2)}) %collective-permute-start.2) | collective-permute-done | bytes 49184 | tf_op jit(solution)/shard_map/ppermute | solution.py:269
  39.3 1.6 %collective-permute-start.3 = (bf16[128,768]{1,0:T(8,128)(2,1)S(1)}, bf16[128,768]{1,0:T(8,128)(2,1)S(1)}, u32[]{:S(2)}, u32[]{:S(2)}) collective-permute-start(bf16[128,768]{1,0:T(8,128)(2,1)S(1)} %get-tuple-element.14), channel_id=1, source_target_pairs={{0,2},{1,3},{2,0},{3,1},{4,6},{5,7},{6,4},{7,5},{8,10},{9,11},{10,... | collective-permute-start | bytes 589832 | tf_op jit(solution)/shard_map/ppermute | solution.py:269
  40.8 1.5 %collective-permute-start.4 = (bf16[128,768]{1,0:T(8,128)(2,1)S(1)}, bf16[128,768]{1,0:T(8,128)(2,1)S(1)}, u32[]{:S(2)}, u32[]{:S(2)}) collective-permute-start(bf16[128,768]{1,0:T(8,128)(2,1)S(1)} %get-tuple-element.14), channel_id=1, source_target_pairs={{0,4},{1,5},{2,6},{3,7},{4,0},{5,1},{6,2},{7,3},{8,12},{9,13},{10,... | collective-permute-start | bytes 589832 | tf_op jit(solution)/shard_map/ppermute | solution.py:269
  42.3 0.0 collective-permute-done.10
  42.3 2.1 %collective-permute-start.5 = (bf16[128,768]{1,0:T(8,128)(2,1)S(1)}, bf16[128,768]{1,0:T(8,128)(2,1)S(1)}, u32[]{:S(2)}, u32[]{:S(2)}) collective-permute-start(bf16[128,768]{1,0:T(8,128)(2,1)S(1)} %get-tuple-element.14), channel_id=1, source_target_pairs={{0,6},{1,7},{2,4},{3,5},{4,2},{5,3},{6,0},{7,1},{8,14},{9,15},{10,... | collective-permute-start | bytes 589832 | tf_op jit(solution)/shard_map/ppermute | solution.py:269
  44.5 1.5 %collective-permute-done.11 = bf16[128,768]{1,0:T(8,128)(2,1)S(1)} collective-permute-done((bf16[128,768]{1,0:T(8,128)(2,1)S(1)}, bf16[128,768]{1,0:T(8,128)(2,1)S(1)}, u32[]{:S(2)}, u32[]{:S(2)}) %collective-permute-start.11) | collective-permute-done | bytes 196640 | tf_op jit(solution)/shard_map/ppermute | solution.py:269
  46.0 1.3 %collective-permute-done.12 = bf16[128,768]{1,0:T(8,128)(2,1)S(1)} collective-permute-done((bf16[128,768]{1,0:T(8,128)(2,1)S(1)}, bf16[128,768]{1,0:T(8,128)(2,1)S(1)}, u32[]{:S(2)}, u32[]{:S(2)}) %collective-permute-start.12) | collective-permute-done | bytes 196640 | tf_op jit(solution)/shard_map/ppermute | solution.py:269
  47.3 0.1 collective-permute-start.13
  47.4 2.7 %collective-permute-done.3 = bf16[128,768]{1,0:T(8,128)(2,1)S(1)} collective-permute-done((bf16[128,768]{1,0:T(8,128)(2,1)S(1)}, bf16[128,768]{1,0:T(8,128)(2,1)S(1)}, u32[]{:S(2)}, u32[]{:S(2)}) %collective-permute-start.3) | collective-permute-done | bytes 196640 | tf_op jit(solution)/shard_map/ppermute | solution.py:269
  50.1 3.3 %collective-permute-done.4 = bf16[128,768]{1,0:T(8,128)(2,1)S(1)} collective-permute-done((bf16[128,768]{1,0:T(8,128)(2,1)S(1)}, bf16[128,768]{1,0:T(8,128)(2,1)S(1)}, u32[]{:S(2)}, u32[]{:S(2)}) %collective-permute-start.4) | collective-permute-done | bytes 196640 | tf_op jit(solution)/shard_map/ppermute | solution.py:269
  53.5 0.0 collective-permute-done.5
  53.5 0.1 collective-permute-start.6
  53.6 0.0 collective-permute-done.13.texts_b
  53.6 2.3 %collective-permute-done.6.images_b = bf16[512,768]{1,0:T(8,128)(2,1)S(1)} collective-permute-done((bf16[512,768]{1,0:T(8,128)(2,1)S(1)}, bf16[512,768]{1,0:T(8,128)(2,1)S(1)}, u32[]{:S(2)}, u32[]{:S(2)}) %collective-permute-start.6) | collective-permute-done | bytes 786464 | tf_op jit(solution)/shard_map/ppermute | solution.py:269
  55.9 0.0 copy-start
  55.9 0.8 %copy-done = bf16[32,768]{1,0:T(8,128)(2,1)S(1)} copy-done((bf16[32,768]{1,0:T(8,128)(2,1)S(1)}, bf16[32,768]{1,0:T(8,128)(2,1)}, u32[]{:S(2)}) %copy-start) | copy-done | bytes 49176
  56.7 9.9 %loss.1 = (f32[32,768]{1,0:T(8,128)}, f32[32,768]{1,0:T(8,128)}) custom-call(bf16[512,768]{1,0:T(8,128)(2,1)S(1)} %constant_dynamic-update-slice_fusion.4.images_a, bf16[512,768]{1,0:T(8,128)(2,1)S(1)} %collective-permute-done.6.images_b, bf16[512,768]{1,0:T(8,128)(2,1)S(1)} %constant_dynamic-update-slice_fusion.15.texts_a, ...), custom_call_target="tpu_custom_call" | custom-call | flops 1610612736 | bytes 3145728 | tf_op jit(solution)/shard_map/loss/pallas_call | solution.py:248
  (13 shorter events, 0.1 us)
Async XLA Ops:
  6.7 21.4 %copy-start.1 = (bf16[32,768]{1,0:T(8,128)(2,1)S(1)}, bf16[32,768]{1,0:T(8,128)(2,1)}, u32[]{:S(2)}) copy-start(bf16[32,768]{1,0:T(8,128)(2,1)} %param.11) | copy-start | bytes 147460
  22.4 10.9 %collective-permute-start.7 = (bf16[32,768]{1,0:T(8,128)(2,1)}, bf16[32,768]{1,0:T(8,128)(2,1)S(1)}, u32[]{:S(2)}, u32[]{:S(2)}) collective-permute-start(bf16[32,768]{1,0:T(8,128)(2,1)} %get-tuple-element.4), channel_id=1, source_target_pairs={{0,8},{1,9},{2,10},{3,11},{4,12},{5,13},{6,14},{7,15},{8,0},{9,1},... | collective-permute-start | bytes 147464 | tf_op jit(solution)/shard_map/ppermute | solution.py:269
  25.5 7.9 %collective-permute-start.8 = (bf16[32,768]{1,0:T(8,128)(2,1)}, bf16[32,768]{1,0:T(8,128)(2,1)S(1)}, u32[]{:S(2)}, u32[]{:S(2)}) collective-permute-start(bf16[32,768]{1,0:T(8,128)(2,1)} %get-tuple-element.4), channel_id=1, source_target_pairs={{0,16},{1,17},{2,18},{3,19},{4,20},{5,21},{6,22},{7,23},{8,24},{9,... | collective-permute-start | bytes 147464 | tf_op jit(solution)/shard_map/ppermute | solution.py:269
  28.1 6.1 %collective-permute-start.9 = (bf16[32,768]{1,0:T(8,128)(2,1)}, bf16[32,768]{1,0:T(8,128)(2,1)S(1)}, u32[]{:S(2)}, u32[]{:S(2)}) collective-permute-start(bf16[32,768]{1,0:T(8,128)(2,1)} %get-tuple-element.4), channel_id=1, source_target_pairs={{0,24},{1,25},{2,26},{3,27},{4,28},{5,29},{6,30},{7,31},{8,16},{9,... | collective-permute-start | bytes 147464 | tf_op jit(solution)/shard_map/ppermute | solution.py:269
  28.1 9.2 %collective-permute-start = (bf16[32,768]{1,0:T(8,128)(2,1)S(1)}, bf16[32,768]{1,0:T(8,128)(2,1)S(1)}, u32[]{:S(2)}, u32[]{:S(2)}) collective-permute-start(bf16[32,768]{1,0:T(8,128)(2,1)S(1)} %copy-done.1), channel_id=1, source_target_pairs={{0,8},{1,9},{2,10},{3,11},{4,12},{5,13},{6,14},{7,15},{8,0},{9,1},... | collective-permute-start | bytes 147464 | tf_op jit(solution)/shard_map/ppermute | solution.py:269
  29.0 8.8 %collective-permute-start.1 = (bf16[32,768]{1,0:T(8,128)(2,1)S(1)}, bf16[32,768]{1,0:T(8,128)(2,1)S(1)}, u32[]{:S(2)}, u32[]{:S(2)}) collective-permute-start(bf16[32,768]{1,0:T(8,128)(2,1)S(1)} %copy-done.1), channel_id=1, source_target_pairs={{0,16},{1,17},{2,18},{3,19},{4,20},{5,21},{6,22},{7,23},{8,24},{9,... | collective-permute-start | bytes 147464 | tf_op jit(solution)/shard_map/ppermute | solution.py:269
  33.3 6.0 %collective-permute-start.2 = (bf16[32,768]{1,0:T(8,128)(2,1)S(1)}, bf16[32,768]{1,0:T(8,128)(2,1)S(1)}, u32[]{:S(2)}, u32[]{:S(2)}) collective-permute-start(bf16[32,768]{1,0:T(8,128)(2,1)S(1)} %copy-done.1), channel_id=1, source_target_pairs={{0,24},{1,25},{2,26},{3,27},{4,28},{5,29},{6,30},{7,31},{8,16},{9,... | collective-permute-start | bytes 147464 | tf_op jit(solution)/shard_map/ppermute | solution.py:269
  34.2 8.2 %collective-permute-start.10 = (bf16[128,768]{1,0:T(8,128)(2,1)S(1)}, bf16[128,768]{1,0:T(8,128)(2,1)S(1)}, u32[]{:S(2)}, u32[]{:S(2)}) collective-permute-start(bf16[128,768]{1,0:T(8,128)(2,1)S(1)} %get-tuple-element.6), channel_id=1, source_target_pairs={{0,2},{1,3},{2,0},{3,1},{4,6},{5,7},{6,4},{7,5},{8,10},{9,11},{10,... | collective-permute-start | bytes 589832 | tf_op jit(solution)/shard_map/ppermute | solution.py:269
  35.7 10.2 %collective-permute-start.11 = (bf16[128,768]{1,0:T(8,128)(2,1)S(1)}, bf16[128,768]{1,0:T(8,128)(2,1)S(1)}, u32[]{:S(2)}, u32[]{:S(2)}) collective-permute-start(bf16[128,768]{1,0:T(8,128)(2,1)S(1)} %get-tuple-element.6), channel_id=1, source_target_pairs={{0,4},{1,5},{2,6},{3,7},{4,0},{5,1},{6,2},{7,3},{8,12},{9,13},{10,... | collective-permute-start | bytes 589832 | tf_op jit(solution)/shard_map/ppermute | solution.py:269
  37.3 10.0 %collective-permute-start.12 = (bf16[128,768]{1,0:T(8,128)(2,1)S(1)}, bf16[128,768]{1,0:T(8,128)(2,1)S(1)}, u32[]{:S(2)}, u32[]{:S(2)}) collective-permute-start(bf16[128,768]{1,0:T(8,128)(2,1)S(1)} %get-tuple-element.6), channel_id=1, source_target_pairs={{0,6},{1,7},{2,4},{3,5},{4,2},{5,3},{6,0},{7,1},{8,14},{9,15},{10,... | collective-permute-start | bytes 589832 | tf_op jit(solution)/shard_map/ppermute | solution.py:269
  39.3 10.9 %collective-permute-start.3 = (bf16[128,768]{1,0:T(8,128)(2,1)S(1)}, bf16[128,768]{1,0:T(8,128)(2,1)S(1)}, u32[]{:S(2)}, u32[]{:S(2)}) collective-permute-start(bf16[128,768]{1,0:T(8,128)(2,1)S(1)} %get-tuple-element.14), channel_id=1, source_target_pairs={{0,2},{1,3},{2,0},{3,1},{4,6},{5,7},{6,4},{7,5},{8,10},{9,11},{10,... | collective-permute-start | bytes 589832 | tf_op jit(solution)/shard_map/ppermute | solution.py:269
  40.8 12.7 %collective-permute-start.4 = (bf16[128,768]{1,0:T(8,128)(2,1)S(1)}, bf16[128,768]{1,0:T(8,128)(2,1)S(1)}, u32[]{:S(2)}, u32[]{:S(2)}) collective-permute-start(bf16[128,768]{1,0:T(8,128)(2,1)S(1)} %get-tuple-element.14), channel_id=1, source_target_pairs={{0,4},{1,5},{2,6},{3,7},{4,0},{5,1},{6,2},{7,3},{8,12},{9,13},{10,... | collective-permute-start | bytes 589832 | tf_op jit(solution)/shard_map/ppermute | solution.py:269
  42.3 11.1 %collective-permute-start.5 = (bf16[128,768]{1,0:T(8,128)(2,1)S(1)}, bf16[128,768]{1,0:T(8,128)(2,1)S(1)}, u32[]{:S(2)}, u32[]{:S(2)}) collective-permute-start(bf16[128,768]{1,0:T(8,128)(2,1)S(1)} %get-tuple-element.14), channel_id=1, source_target_pairs={{0,6},{1,7},{2,4},{3,5},{4,2},{5,3},{6,0},{7,1},{8,14},{9,15},{10,... | collective-permute-start | bytes 589832 | tf_op jit(solution)/shard_map/ppermute | solution.py:269
  47.3 6.3 %collective-permute-start.13 = (bf16[512,768]{1,0:T(8,128)(2,1)S(1)}, bf16[512,768]{1,0:T(8,128)(2,1)S(1)}, u32[]{:S(2)}, u32[]{:S(2)}) collective-permute-start(bf16[512,768]{1,0:T(8,128)(2,1)S(1)} %constant_dynamic-update-slice_fusion.15.texts_a), channel_id=1, source_target_pairs={{0,1},{1,0},{2,3},{3,2},{4,5},{5,4},{6,7},{7,6},{8,9},{9,8},{10,11... | collective-permute-start | bytes 2359304 | tf_op jit(solution)/shard_map/ppermute | solution.py:269
  53.5 2.4 %collective-permute-start.6 = (bf16[512,768]{1,0:T(8,128)(2,1)S(1)}, bf16[512,768]{1,0:T(8,128)(2,1)S(1)}, u32[]{:S(2)}, u32[]{:S(2)}) collective-permute-start(bf16[512,768]{1,0:T(8,128)(2,1)S(1)} %constant_dynamic-update-slice_fusion.4.images_a), channel_id=1, source_target_pairs={{0,1},{1,0},{2,3},{3,2},{4,5},{5,4},{6,7},{7,6},{8,9},{9,8},{10,11... | collective-permute-start | bytes 2359304 | tf_op jit(solution)/shard_map/ppermute | solution.py:269
  55.9 0.8 %copy-start = (bf16[32,768]{1,0:T(8,128)(2,1)S(1)}, bf16[32,768]{1,0:T(8,128)(2,1)}, u32[]{:S(2)}) copy-start(bf16[32,768]{1,0:T(8,128)(2,1)} %get-tuple-element.5.embed) | copy-start | bytes 147460

commit v2 on v1

v2 whole, which is shorter than its diff:
```python
import functools
import math

import jax
import jax.numpy as jnp
from jax import lax
from jax.experimental import pallas as pl
from jax.experimental.pallas import tpu as pltpu
from jax.sharding import PartitionSpec as P


HEADS = 12
GROUP = 8
LOGIT_SCALE = 100.0
EPS_NORM = 1e-05
EPS_UNIT = 1e-06
BF16 = jnp.bfloat16
F32 = jnp.float32
MIB = 1024 * 1024
UNIT_FLOPS = 4 * 10**9


def layer_norm(values):
    center = values - jnp.mean(values, axis=-1, keepdims=True)
    spread = jnp.mean(center * center, axis=-1, keepdims=True)
    return center * lax.rsqrt(spread + EPS_NORM)


def inverse_norm(values):
    return lax.rsqrt(jnp.sum(values * values, axis=-1, keepdims=True) + EPS_UNIT)


def dot(left, right):
    return jnp.dot(left, right, preferred_element_type=F32)


def dot_last(left, right):
    return lax.dot_general(left, right, (((1,), (1,)), ((), ())), preferred_element_type=F32)


def erf(x):
    x = jnp.clip(x, -3.832506856900711, 3.832506856900711)
    y = x * x
    top = jnp.full_like(x, 0.00022905065861350646)
    for c in (
        0.0034082910107109506,
        0.050955695062380861,
        0.18520832239976145,
        1.128379143519084,
    ):
        top = top * y + c
    bottom = jnp.full_like(x, -1.1791602954361697e-7)
    for c in (
        0.000023547966471313185,
        0.0010179625278914885,
        0.014070470171167667,
        0.11098505178285362,
        0.49746925110067538,
        1.0,
    ):
        bottom = bottom * y + c
    return x * top / bottom


def attend_kernel(
    layout, caps, w_query, w_keyval, w_out, residual_ref, normed, mapped, mix, key, limits
):
    context, count, width = caps.shape
    groups = count // GROUP
    slots = normed.shape[1]
    head_dim = width // HEADS
    base = lax.axis_index("dp") * count
    lengths = [layout[0, base + c] for c in range(count)]
    ends = [jnp.clip(length - 1, 0, context - 1) for length in lengths]

    rows = GROUP * HEADS
    lane = lax.broadcasted_iota(jnp.int32, (rows, slots), 1)
    line = lax.broadcasted_iota(jnp.int32, (rows, slots), 0)
    key[...] = jnp.where(lane % GROUP == line % GROUP, lane // GROUP, context)
    owner = lax.broadcasted_iota(jnp.int32, (rows, 128), 0) % GROUP
    for g in range(groups):
        limit = jnp.full((rows, 128), 0, jnp.int32)
        for k in range(GROUP):
            limit = jnp.where(owner == k, lengths[g * GROUP + k], limit)
        limits[g] = limit
        normed[g, :, width:] = jnp.ones((slots, 128), BF16)
    pair = 2 * GROUP
    done = (context + 1) // 2 * pair

    def normalise(g):
        for t in range(context // 2):
            value = caps[pl.ds(2 * t, 2), pl.ds(g * GROUP, GROUP)].astype(F32).reshape(pair, width)
            normed[g, pl.ds(t * pair, pair), :width] = layer_norm(value).astype(BF16)
        if context % 2:
            tail = layer_norm(caps[context - 1, pl.ds(g * GROUP, GROUP)].astype(F32))
            tail = jnp.concatenate([tail, jnp.zeros((GROUP, width), F32)], axis=0)
            normed[g, pl.ds(context // 2 * pair, pair), :width] = tail.astype(BF16)
        if done < slots:
            normed[g, pl.ds(done, slots - done), :width] = jnp.zeros((slots - done, width), BF16)

    normalise(0)
    row = lax.broadcasted_iota(jnp.int32, (GROUP, width), 0)
    tokens = []
    for g in range(groups):
        part = pl.ds(g * GROUP, GROUP)
        lines = [caps[ends[g * GROUP + k], part].astype(F32) for k in range(GROUP)]
        token = lines[0]
        for k in range(1, GROUP):
            token = jnp.where(row == k, lines[k], token)
        tokens.append(token)
    tokens = jnp.concatenate(tokens, axis=0)
    end_normed = layer_norm(tokens).astype(BF16)
    query = dot(end_normed, w_query[...]).astype(BF16).astype(F32)
    normalise(1)
    head_of = lax.broadcasted_iota(jnp.int32, (count, width), 1) // head_dim
    spread = [jnp.where(head_of == h, query, 0.0) for h in range(HEADS)]
    spread = jnp.concatenate(spread, axis=0).astype(BF16)
    scale = 1.0 / math.sqrt(head_dim)
    mapped[...] = (dot_last(spread, w_keyval[:, :width]) * scale).reshape(mapped.shape)

    def attend(g, score):
        limit = jnp.concatenate([limits[g]] * (slots // 128), axis=1)
        masked = jnp.where(key[...] < limit, score, -jnp.inf)
        exponent = jnp.exp(masked - jnp.max(masked, axis=-1, keepdims=True))
        values = dot(exponent.astype(BF16), normed[g])
        mass = jnp.concatenate([values[:, width:]] * (width // 128), axis=1)
        values = values[:, :width] / mass
        mix[:, pl.ds(g * GROUP, GROUP), :] = values.reshape(HEADS, GROUP, width)

    for g in range(2, groups):
        normalise(g)
    scores = []
    for g in range(groups):
        mine = mapped[:, pl.ds(g * GROUP, GROUP), :].reshape(rows, width).astype(BF16)
        scores.append(dot_last(mine, normed[g, :, :width]))
    for g in range(groups):
        attend(g, scores[g])
    mixed = dot(mix[...].reshape(HEADS * count, width).astype(BF16), w_keyval[:, width:])
    picked = mixed[:count]
    for h in range(1, HEADS):
        picked = jnp.where(head_of == h, mixed[h * count : (h + 1) * count], picked)
    residual_ref[...] = (tokens + dot(picked.astype(BF16), w_out[...])).astype(BF16)


def attend(layout, captions, weights):
    count, context, width = captions.shape
    groups = count // GROUP
    slots = -(-context * GROUP // 128) * 128
    flops = 2 * count * width * (5 * width + 2 * HEADS * slots)
    return pl.pallas_call(
        attend_kernel,
        out_shape=jax.ShapeDtypeStruct((count, width), BF16),
        in_specs=[pl.BlockSpec(memory_space=pltpu.SMEM)]
        + [pl.BlockSpec(memory_space=pltpu.VMEM)] * 4,
        out_specs=pl.BlockSpec(memory_space=pltpu.VMEM),
        scratch_shapes=[
            pltpu.VMEM((groups, slots, width + 128), BF16),
            pltpu.VMEM((HEADS, count, width), F32),
            pltpu.VMEM((HEADS, count, width), F32),
            pltpu.VMEM((GROUP * HEADS, slots), jnp.int32),
            pltpu.VMEM((groups, GROUP * HEADS, 128), jnp.int32),
        ],
        compiler_params=pltpu.CompilerParams(vmem_limit_bytes=20 * MIB),
        cost_estimate=pl.CostEstimate(
            flops=8 * flops,
            bytes_accessed=2 * captions.size + 8 * width * width,
            transcendentals=count * HEADS * slots,
        ),
        name="attend",
    )(layout, jnp.transpose(captions, (1, 0, 2)), *weights)


def unit_kernel(images, units):
    value = images[...].astype(F32)
    units[...] = (value * inverse_norm(value)).astype(BF16)


def unit_rows(images):
    return pl.pallas_call(
        unit_kernel,
        out_shape=jax.ShapeDtypeStruct(images.shape, BF16),
        in_specs=[pl.BlockSpec(memory_space=pltpu.VMEM)],
        out_specs=pl.BlockSpec(memory_space=pltpu.VMEM),
        compiler_params=pltpu.CompilerParams(vmem_limit_bytes=4 * MIB),
        cost_estimate=pl.CostEstimate(
            flops=UNIT_FLOPS, bytes_accessed=4 * images.size, transcendentals=0
        ),
        name="unit",
    )(images)


def forward_kernel(residual_ref, w_up, w_down, w_proj, units_ref, embed_ref):
    residual = residual_ref[...].astype(F32)
    inner = layer_norm(residual).astype(BF16)
    hidden = dot(inner, w_up[...])
    hidden = (0.5 * hidden * (1.0 + erf(hidden * math.sqrt(0.5)))).astype(BF16)
    final = residual + dot(hidden, w_down[...])
    pooled = layer_norm(final).astype(BF16)
    embed = dot(pooled, w_proj[...]).astype(BF16)
    embed_ref[...] = embed
    embed = embed.astype(F32)
    units_ref[...] = (embed * inverse_norm(embed)).astype(BF16)


def forward(residual, weights):
    result = jax.ShapeDtypeStruct((residual.shape[0], weights[2].shape[1]), BF16)
    size = sum(w.size for w in weights)
    return pl.pallas_call(
        forward_kernel,
        out_shape=(result, result),
        in_specs=[pl.BlockSpec(memory_space=pltpu.VMEM)] * 4,
        out_specs=(pl.BlockSpec(memory_space=pltpu.VMEM),) * 2,
        compiler_params=pltpu.CompilerParams(vmem_limit_bytes=8 * MIB),
        cost_estimate=pl.CostEstimate(
            flops=4 * residual.shape[0] * size, bytes_accessed=2 * size, transcendentals=0
        ),
        name="forward",
    )(residual, *weights)


def unit_grad(grad, value):
    inverse = inverse_norm(value)
    inner = jnp.sum(value * grad, axis=-1, keepdims=True)
    return grad * inverse - value * (inner * inverse * inverse * inverse)


def lse_steps(tile, rows_of, columns, after):
    total, width = rows_of.shape[0], columns.shape[0]

    def score_tile(i):
        return LOGIT_SCALE * dot_last(rows_of[pl.ds(i * tile, tile), :], columns[...])

    def step(i, s, carry):
        top, mass = carry
        peak = jnp.max(s, axis=1, keepdims=True)
        after(pl.ds(i * tile, tile), s, peak, jnp.sum(jnp.exp(s - peak), axis=1, keepdims=True))
        higher = jnp.maximum(top, jnp.max(s, axis=0, keepdims=True))
        mass = mass * jnp.exp(top - higher) + jnp.sum(jnp.exp(s - higher), axis=0, keepdims=True)
        return higher, mass

    ends = (jnp.full((1, width), -jnp.inf, F32), jnp.zeros((1, width), F32))
    if total // tile <= 4:
        score = score_tile(0)
        for i in range(total // tile):
            following = score_tile(i + 1) if i + 1 < total // tile else None
            ends = step(i, score, ends)
            score = following
    else:
        ends = lax.fori_loop(0, total // tile, lambda i, c: step(i, score_tile(i), c), ends)
    return ends[0] + jnp.log(ends[1])


def loss_kernel(
    images_a,
    images_b,
    texts_a,
    texts_b,
    images,
    embed,
    image_out,
    text_out,
    pictures,
    texts,
    sides,
    row_lse,
    *,
    tile,
):
    half = images_a.shape[0]
    count = images.shape[0]
    pictures[:half, :] = images_a[...]
    pictures[half:, :] = images_b[...]
    texts[:half, :] = texts_a[...]
    texts[half:, :] = texts_b[...]

    def after(rows, s, peak, mass):
        sides[rows, :] = s[:, :128]
        row_lse[rows, :] = jnp.broadcast_to(peak + jnp.log(mass), (tile, 128))

    column_lse = lse_steps(tile, pictures, texts, after)

    def product(weights, other):
        both = dot(jnp.concatenate(weights, axis=0), other[...])
        return (0.5 * LOGIT_SCALE) * (both[:count] + both[count:])

    score = LOGIT_SCALE * dot_last(pictures[:count, :], texts[...])
    weights = [
        jnp.exp(score - row_lse[:count, :1]).astype(BF16),
        jnp.exp(score - column_lse).astype(BF16),
    ]
    image_grad = product(weights, texts) - LOGIT_SCALE * texts[:count, :].astype(F32)
    side = sides[...]
    weights = [
        jnp.exp(side - row_lse[...]).T[:count].astype(BF16),
        jnp.exp(side - column_lse[:, :128]).T[:count].astype(BF16),
    ]
    text_grad = product(weights, pictures) - LOGIT_SCALE * pictures[:count, :].astype(F32)
    image_out[...] = unit_grad(image_grad, images[...].astype(F32))
    text_out[...] = unit_grad(text_grad, embed[...].astype(F32))


def loss(pictures, texts, images, embed):
    half, width = pictures[0].shape
    total = 2 * half
    result = jax.ShapeDtypeStruct(images.shape, F32)
    return pl.pallas_call(
        functools.partial(loss_kernel, tile=256),
        out_shape=(result, result),
        in_specs=[pl.BlockSpec(memory_space=pltpu.VMEM)] * 6,
        out_specs=(pl.BlockSpec(memory_space=pltpu.VMEM),) * 2,
        scratch_shapes=[
            pltpu.VMEM((total, width), BF16),
            pltpu.VMEM((total, width), BF16),
            pltpu.VMEM((total, 128), F32),
            pltpu.VMEM((total, 128), F32),
        ],
        compiler_params=pltpu.CompilerParams(vmem_limit_bytes=40 * MIB),
        cost_estimate=pl.CostEstimate(
            flops=2 * total * total * width,
            bytes_accessed=4 * total * width,
            transcendentals=2 * total * total,
        ),
        name="loss",
    )(*pictures, *texts, images, embed)


def exchange(value, mask):
    devices = range(lax.axis_size("dp"))
    return lax.ppermute(value, "dp", [(i, i ^ mask) for i in devices])


def digit_masks(devices):
    groups, high = [], devices
    while high > 2:
        low = max(high // 4, 2)
        groups.append([k * low for k in range(1, high // low)])
        high = low
    return groups


def gather(value):
    for masks in digit_masks(lax.axis_size("dp")):
        parts = []
        for mask in masks:
            parts.append(exchange(value, mask))
        value, *parts = lax.optimization_barrier((value, *parts))
        value = jnp.concatenate([value, *parts], axis=0)
    return value, exchange(value, 1)


def body(captions, layout, images, w_query, w_keyval, w_out, w_up, w_down, w_proj):
    image_units = unit_rows(images)
    pictures = gather(image_units)
    residual = attend(layout, captions, (w_query, w_keyval, w_out))
    text_units, embed = forward(residual, (w_up, w_down, w_proj))
    texts = gather(text_units)
    return loss(pictures, texts, images, embed)


def solution(mesh):
    return jax.shard_map(
        body,
        mesh=mesh,
        in_specs=(P("dp", None, None), P(), P("dp", None), P(), P(), P(), P(), P(), P()),
        out_specs=(P("dp", None), P("dp", None)),
        check_vma=False,
    )
```

time: 66.9 us -> 54.2 us (0.81)
  Pallas kernels: 25.6 us -> 12.9 us
    pallas_call x2 -> x4, Pallas kernels: 25.6 us -> 12.9 us  [the longest x1 5.76 us: attend(): pl.pallas_call(attend_kernel, out_shape=jax.ShapeDtypeStruct((count, widt...]
    ppermute x14, waiting for transfers between devices: 13.4 us -> 14 us  [exchange(): return lax.ppermute(value, 'dp', [(i, i ^ mask) for i in devices])]
    unnamed x15 -> x30, local copies, waits for them, and re-layouts: 7.73 us -> 7.11 us
  transfers between devices with their start and end apart: 14 -> 14, of which waited for: 7 -> 8; matrix products, arithmetic and copies ran while one was open for 1% -> 0% of each run, Pallas kernels for 0% -> 0%
where the time goes in v2:
time: 54.2 us; the launch traced here: 53.9 us
  starting transfers between devices  18.9 us (35%)
  waiting for transfers between devices  14 us (26%)
  Pallas kernels  12.9 us (24%)
  local copies, waits for them, and re-layouts  7.15 us (13%)
  between operations  0.83 us (2%)
    ppermute x14, starting transfers between devices, exchange(): return lax.ppermute(value, 'dp', [(i, i ^ mask) for i in devices])  18.9 us
    ppermute x14, waiting for transfers between devices, exchange(): return lax.ppermute(value, 'dp', [(i, i ^ mask) for i in devices])  14 us
    unnamed x30, local copies, waits for them, and re-layouts  7.11 us
    pallas_call x1, Pallas kernels, attend(): pl.pallas_call(attend_kernel, out_shape=jax.ShapeDtypeStruct((count, widt...  5.76 us
    pallas_call x1, Pallas kernels, loss(): pl.pallas_call(functools.partial(loss_kernel, tile=256), out_shape=(resul...  4.38 us
    pallas_call x1, Pallas kernels, forward(): pl.pallas_call(forward_kernel, out_shape=(result, result), in_specs=[pl.B...  2.7 us
  transfers between devices with their start and end apart: 14, of which 8 were waited for; matrix products, arithmetic and copies ran while one was open for 0% of the time, Pallas kernels for 0%

profile of v2, /device:TPU:0, one launch (start us, length us, event | category | flops | bytes accessed | tf_op | source)
XLA Modules:
  0.0 53.9 jit_solution(18394781150465546036)
XLA Ops:
  0.6 0.0 copy-start.3
  0.6 2.1 %copy-done.3 = bf16[32,77,768]{2,0,1:T(8,128)(2,1)S(1)} copy-done((bf16[32,77,768]{2,0,1:T(8,128)(2,1)S(1)}, bf16[32,77,768]{2,0,1:T(8,128)(2,1)}, u32[]{:S(2)}) %copy-start.3) | copy-done | bytes 3784728
  2.7 0.0 copy-start.4
  2.7 1.7 %copy-done.4 = bf16[768,1536]{1,0:T(8,128)(2,1)S(1)} copy-done((bf16[768,1536]{1,0:T(8,128)(2,1)S(1)}, bf16[768,1536]{1,0:T(8,128)(2,1)}, u32[]{:S(2)}) %copy-start.4) | copy-done | bytes 2359320
  4.4 0.0 copy-start.5
  4.4 1.3 %copy-done.5 = bf16[768,768]{1,0:T(8,128)(2,1)S(1)} copy-done((bf16[768,768]{1,0:T(8,128)(2,1)S(1)}, bf16[768,768]{1,0:T(8,128)(2,1)}, u32[]{:S(2)}) %copy-start.5) | copy-done | bytes 1179672
  5.6 0.0 copy-start.6
  5.6 1.3 %copy-done.6 = bf16[768,768]{1,0:T(8,128)(2,1)S(1)} copy-done((bf16[768,768]{1,0:T(8,128)(2,1)S(1)}, bf16[768,768]{1,0:T(8,128)(2,1)}, u32[]{:S(2)}) %copy-start.6) | copy-done | bytes 1179672
  6.9 0.0 copy-start.8
  6.9 0.7 %copy-done.8 = s32[2,1024]{1,0:T(2,128)S(1)} copy-done((s32[2,1024]{1,0:T(2,128)S(1)}, s32[2,1024]{1,0:T(2,128)}, u32[]{:S(2)}) %copy-start.8) | copy-done | bytes 8216
  7.6 0.0 copy-start
  7.6 5.8 %attend.1.residual_ref = bf16[32,768]{1,0:T(8,128)(2,1)S(1)} custom-call(s32[2,1024]{1,0:T(2,128)S(1)} %copy-done.8, bf16[77,32,768]{2,1,0:T(8,128)(2,1)S(1)} %bitcast.1, bf16[768,768]{1,0:T(8,128)(2,1)S(1)} %copy-done.5, bf16[768,1536]{1,0:T(8,128)(2,1)S(1)} %copy-done.4, bf16[768,768]{1,0:T(8,128)(2,1)S(1)} %copy-done.6), custom_call_target="tpu_custom_call" | custom-call | flops 7549747200 | bytes 8503296 | tf_op jit(solution)/shard_map/attend/pallas_call | solution.py:150
  13.4 0.0 copy-done
  13.4 0.0 copy-done.1
  13.4 0.0 copy-done.2
  13.4 0.0 copy-start.7
  13.4 2.7 %forward.1 = (bf16[32,768]{1,0:T(8,128)(2,1)S(1)}, bf16[32,768]{1,0:T(8,128)(2,1)S(1)}) custom-call(bf16[32,768]{1,0:T(8,128)(2,1)S(1)} %attend.1.residual_ref, bf16[768,3072]{1,0:T(8,128)(2,1)S(1)} %copy-done, bf16[3072,768]{1,0:T(8,128)(2,1)S(1)} %copy-done.1, bf16[768,768]{1,0:T(8,128)(2,1)S(1)} %copy-done.2), custom_call_target="tpu_custom_call" | custom-call | flops 679477248 | bytes 10616832 | tf_op jit(solution)/shard_map/forward/pallas_call | solution.py:208
  16.1 5.1 %collective-permute-start.9 = (bf16[32,768]{1,0:T(8,128)(2,1)S(1)}, bf16[32,768]{1,0:T(8,128)(2,1)S(1)}, u32[]{:S(2)}, u32[]{:S(2)}) collective-permute-start(bf16[32,768]{1,0:T(8,128)(2,1)S(1)} %get-tuple-element.29), channel_id=1, source_target_pairs={{0,24},{1,25},{2,26},{3,27},{4,28},{5,29},{6,30},{7,31},{8,16},{9,... | collective-permute-start | bytes 147464 | tf_op jit(solution)/shard_map/ppermute | solution.py:329
  21.3 0.0 collective-permute-start.8
  21.3 0.6 %collective-permute-start.7 = (bf16[32,768]{1,0:T(8,128)(2,1)S(1)}, bf16[32,768]{1,0:T(8,128)(2,1)S(1)}, u32[]{:S(2)}, u32[]{:S(2)}) collective-permute-start(bf16[32,768]{1,0:T(8,128)(2,1)S(1)} %get-tuple-element.29), channel_id=1, source_target_pairs={{0,8},{1,9},{2,10},{3,11},{4,12},{5,13},{6,14},{7,15},{8,0},{9,1},... | collective-permute-start | bytes 147464 | tf_op jit(solution)/shard_map/ppermute | solution.py:329
  21.9 0.0 copy-done.7
  21.9 0.1 unit.1
  22.0 3.8 %collective-permute-start.2 = (bf16[32,768]{1,0:T(8,128)(2,1)S(1)}, bf16[32,768]{1,0:T(8,128)(2,1)S(1)}, u32[]{:S(2)}, u32[]{:S(2)}) collective-permute-start(bf16[32,768]{1,0:T(8,128)(2,1)S(1)} %unit.1), channel_id=1, source_target_pairs={{0,24},{1,25},{2,26},{3,27},{4,28},{5,29},{6,30},{7,31},{8,16},{9,... | collective-permute-start | bytes 147464 | tf_op jit(solution)/shard_map/ppermute | solution.py:329
  25.8 0.0 collective-permute-start.1
  25.8 0.0 collective-permute-done.9
  25.8 0.6 %collective-permute-start = (bf16[32,768]{1,0:T(8,128)(2,1)S(1)}, bf16[32,768]{1,0:T(8,128)(2,1)S(1)}, u32[]{:S(2)}, u32[]{:S(2)}) collective-permute-start(bf16[32,768]{1,0:T(8,128)(2,1)S(1)} %unit.1), channel_id=1, source_target_pairs={{0,8},{1,9},{2,10},{3,11},{4,12},{5,13},{6,14},{7,15},{8,0},{9,1},... | collective-permute-start | bytes 147464 | tf_op jit(solution)/shard_map/ppermute | solution.py:329
  26.5 0.9 %collective-permute-done.8 = bf16[32,768]{1,0:T(8,128)(2,1)S(1)} collective-permute-done((bf16[32,768]{1,0:T(8,128)(2,1)S(1)}, bf16[32,768]{1,0:T(8,128)(2,1)S(1)}, u32[]{:S(2)}, u32[]{:S(2)}) %collective-permute-start.8) | collective-permute-done | bytes 49184 | tf_op jit(solution)/shard_map/ppermute | solution.py:329
  27.4 0.0 collective-permute-done.7
  27.4 2.5 %collective-permute-start.12 = (bf16[128,768]{1,0:T(8,128)(2,1)S(1)}, bf16[128,768]{1,0:T(8,128)(2,1)S(1)}, u32[]{:S(2)}, u32[]{:S(2)}) collective-permute-start(bf16[128,768]{1,0:T(8,128)(2,1)S(1)} %constant_dynamic-update-slice_fusion.8), channel_id=1, source_target_pairs={{0,6},{1,7},{2,4},{3,5},{4,2},{5,3},{6,0},{7,1},{8,14},{9,15},{10,... | collective-permute-start | bytes 589832 | tf_op jit(solution)/shard_map/ppermute | solution.py:329
  29.9 0.5 collective-permute-start.11
  30.4 0.0 collective-permute-done.2
  30.4 0.6 %collective-permute-start.10 = (bf16[128,768]{1,0:T(8,128)(2,1)S(1)}, bf16[128,768]{1,0:T(8,128)(2,1)S(1)}, u32[]{:S(2)}, u32[]{:S(2)}) collective-permute-start(bf16[128,768]{1,0:T(8,128)(2,1)S(1)} %constant_dynamic-update-slice_fusion.8), channel_id=1, source_target_pairs={{0,2},{1,3},{2,0},{3,1},{4,6},{5,7},{6,4},{7,5},{8,10},{9,11},{10,... | collective-permute-start | bytes 589832 | tf_op jit(solution)/shard_map/ppermute | solution.py:329
  31.0 0.0 collective-permute-done.1
  31.0 0.0 collective-permute-done
  31.1 2.5 %collective-permute-start.5 = (bf16[128,768]{1,0:T(8,128)(2,1)S(1)}, bf16[128,768]{1,0:T(8,128)(2,1)S(1)}, u32[]{:S(2)}, u32[]{:S(2)}) collective-permute-start(bf16[128,768]{1,0:T(8,128)(2,1)S(1)} %constant_dynamic-update-slice_fusion), channel_id=1, source_target_pairs={{0,6},{1,7},{2,4},{3,5},{4,2},{5,3},{6,0},{7,1},{8,14},{9,15},{10,... | collective-permute-start | bytes 589832 | tf_op jit(solution)/shard_map/ppermute | solution.py:329
  33.5 0.5 collective-permute-start.4
  34.1 2.2 %collective-permute-done.12 = bf16[128,768]{1,0:T(8,128)(2,1)S(1)} collective-permute-done((bf16[128,768]{1,0:T(8,128)(2,1)S(1)}, bf16[128,768]{1,0:T(8,128)(2,1)S(1)}, u32[]{:S(2)}, u32[]{:S(2)}) %collective-permute-start.12) | collective-permute-done | bytes 196640 | tf_op jit(solution)/shard_map/ppermute | solution.py:329
  36.3 1.5 %collective-permute-start.3 = (bf16[128,768]{1,0:T(8,128)(2,1)S(1)}, bf16[128,768]{1,0:T(8,128)(2,1)S(1)}, u32[]{:S(2)}, u32[]{:S(2)}) collective-permute-start(bf16[128,768]{1,0:T(8,128)(2,1)S(1)} %constant_dynamic-update-slice_fusion), channel_id=1, source_target_pairs={{0,2},{1,3},{2,0},{3,1},{4,6},{5,7},{6,4},{7,5},{8,10},{9,11},{10,... | collective-permute-start | bytes 589832 | tf_op jit(solution)/shard_map/ppermute | solution.py:329
  37.7 4.1 %collective-permute-done.11 = bf16[128,768]{1,0:T(8,128)(2,1)S(1)} collective-permute-done((bf16[128,768]{1,0:T(8,128)(2,1)S(1)}, bf16[128,768]{1,0:T(8,128)(2,1)S(1)}, u32[]{:S(2)}, u32[]{:S(2)}) %collective-permute-start.11) | collective-permute-done | bytes 196640 | tf_op jit(solution)/shard_map/ppermute | solution.py:329
  41.9 0.0 collective-permute-done.10
  41.9 2.2 %collective-permute-done.5 = bf16[128,768]{1,0:T(8,128)(2,1)S(1)} collective-permute-done((bf16[128,768]{1,0:T(8,128)(2,1)S(1)}, bf16[128,768]{1,0:T(8,128)(2,1)S(1)}, u32[]{:S(2)}, u32[]{:S(2)}) %collective-permute-start.5) | collective-permute-done | bytes 196640 | tf_op jit(solution)/shard_map/ppermute | solution.py:329
  44.0 1.7 %collective-permute-done.4 = bf16[128,768]{1,0:T(8,128)(2,1)S(1)} collective-permute-done((bf16[128,768]{1,0:T(8,128)(2,1)S(1)}, bf16[128,768]{1,0:T(8,128)(2,1)S(1)}, u32[]{:S(2)}, u32[]{:S(2)}) %collective-permute-start.4) | collective-permute-done | bytes 196640 | tf_op jit(solution)/shard_map/ppermute | solution.py:329
  45.7 0.2 collective-permute-done.3
  46.0 0.1 collective-permute-start.13
  46.1 0.6 %collective-permute-start.6 = (bf16[512,768]{1,0:T(8,128)(2,1)S(1)}, bf16[512,768]{1,0:T(8,128)(2,1)S(1)}, u32[]{:S(2)}, u32[]{:S(2)}) collective-permute-start(bf16[512,768]{1,0:T(8,128)(2,1)S(1)} %constant_dynamic-update-slice_fusion.4.images_a), channel_id=1, source_target_pairs={{0,1},{1,0},{2,3},{3,2},{4,5},{5,4},{6,7},{7,6},{8,9},{9,8},{10,11... | collective-permute-start | bytes 2359304 | tf_op jit(solution)/shard_map/ppermute | solution.py:329
  46.7 1.6 %collective-permute-done.13.texts_b = bf16[512,768]{1,0:T(8,128)(2,1)S(1)} collective-permute-done((bf16[512,768]{1,0:T(8,128)(2,1)S(1)}, bf16[512,768]{1,0:T(8,128)(2,1)S(1)}, u32[]{:S(2)}, u32[]{:S(2)}) %collective-permute-start.13) | collective-permute-done | bytes 786464 | tf_op jit(solution)/shard_map/ppermute | solution.py:329
  48.3 1.1 %collective-permute-done.6.images_b = bf16[512,768]{1,0:T(8,128)(2,1)S(1)} collective-permute-done((bf16[512,768]{1,0:T(8,128)(2,1)S(1)}, bf16[512,768]{1,0:T(8,128)(2,1)S(1)}, u32[]{:S(2)}, u32[]{:S(2)}) %collective-permute-start.6) | collective-permute-done | bytes 786464 | tf_op jit(solution)/shard_map/ppermute | solution.py:329
  49.5 4.4 %loss.1 = (f32[32,768]{1,0:T(8,128)}, f32[32,768]{1,0:T(8,128)}) custom-call(bf16[512,768]{1,0:T(8,128)(2,1)S(1)} %constant_dynamic-update-slice_fusion.4.images_a, bf16[512,768]{1,0:T(8,128)(2,1)S(1)} %collective-permute-done.6.images_b, bf16[512,768]{1,0:T(8,128)(2,1)S(1)} %constant_dynamic-update-slice_fusion.12.texts_a, ...), custom_call_target="tpu_custom_call" | custom-call | flops 1610612736 | bytes 3145728 | tf_op jit(solution)/shard_map/loss/pallas_call | solution.py:306
  (18 shorter events, 0.2 us)
Async XLA Ops:
  0.6 2.1 %copy-start.3 = (bf16[32,77,768]{2,0,1:T(8,128)(2,1)S(1)}, bf16[32,77,768]{2,0,1:T(8,128)(2,1)}, u32[]{:S(2)}) copy-start(bf16[32,77,768]{2,0,1:T(8,128)(2,1)} %param.9) | copy-start | bytes 11354116
  2.7 1.7 %copy-start.4 = (bf16[768,1536]{1,0:T(8,128)(2,1)S(1)}, bf16[768,1536]{1,0:T(8,128)(2,1)}, u32[]{:S(2)}) copy-start(bf16[768,1536]{1,0:T(8,128)(2,1)} %w_keyval.1) | copy-start | bytes 7077892
  4.4 1.3 %copy-start.5 = (bf16[768,768]{1,0:T(8,128)(2,1)S(1)}, bf16[768,768]{1,0:T(8,128)(2,1)}, u32[]{:S(2)}) copy-start(bf16[768,768]{1,0:T(8,128)(2,1)} %w_query.1) | copy-start | bytes 3538948
  5.6 1.3 %copy-start.6 = (bf16[768,768]{1,0:T(8,128)(2,1)S(1)}, bf16[768,768]{1,0:T(8,128)(2,1)}, u32[]{:S(2)}) copy-start(bf16[768,768]{1,0:T(8,128)(2,1)} %w_out.1) | copy-start | bytes 3538948
  6.9 0.7 %copy-start.8 = (s32[2,1024]{1,0:T(2,128)S(1)}, s32[2,1024]{1,0:T(2,128)}, u32[]{:S(2)}) copy-start(s32[2,1024]{1,0:T(2,128)} %layout.1) | copy-start | bytes 24580
  7.6 5.8 %copy-start = (bf16[768,3072]{1,0:T(8,128)(2,1)S(1)}, bf16[768,3072]{1,0:T(8,128)(2,1)}, u32[]{:S(2)}) copy-start(bf16[768,3072]{1,0:T(8,128)(2,1)} %w_up.1) | copy-start | bytes 14155780
  7.6 5.8 %copy-start.1 = (bf16[3072,768]{1,0:T(8,128)(2,1)S(1)}, bf16[3072,768]{1,0:T(8,128)(2,1)}, u32[]{:S(2)}) copy-start(bf16[3072,768]{1,0:T(8,128)(2,1)} %w_down.1) | copy-start | bytes 14155780
  7.6 5.8 %copy-start.2 = (bf16[768,768]{1,0:T(8,128)(2,1)S(1)}, bf16[768,768]{1,0:T(8,128)(2,1)}, u32[]{:S(2)}) copy-start(bf16[768,768]{1,0:T(8,128)(2,1)} %w_proj.1) | copy-start | bytes 3538948
  13.4 8.5 %copy-start.7 = (bf16[32,768]{1,0:T(8,128)(2,1)S(1)}, bf16[32,768]{1,0:T(8,128)(2,1)}, u32[]{:S(2)}) copy-start(bf16[32,768]{1,0:T(8,128)(2,1)} %images.3) | copy-start | bytes 147460
  16.1 9.7 %collective-permute-start.9 = (bf16[32,768]{1,0:T(8,128)(2,1)S(1)}, bf16[32,768]{1,0:T(8,128)(2,1)S(1)}, u32[]{:S(2)}, u32[]{:S(2)}) collective-permute-start(bf16[32,768]{1,0:T(8,128)(2,1)S(1)} %get-tuple-element.29), channel_id=1, source_target_pairs={{0,24},{1,25},{2,26},{3,27},{4,28},{5,29},{6,30},{7,31},{8,16},{9,... | collective-permute-start | bytes 147464 | tf_op jit(solution)/shard_map/ppermute | solution.py:329
  21.3 6.1 %collective-permute-start.8 = (bf16[32,768]{1,0:T(8,128)(2,1)S(1)}, bf16[32,768]{1,0:T(8,128)(2,1)S(1)}, u32[]{:S(2)}, u32[]{:S(2)}) collective-permute-start(bf16[32,768]{1,0:T(8,128)(2,1)S(1)} %get-tuple-element.29), channel_id=1, source_target_pairs={{0,16},{1,17},{2,18},{3,19},{4,20},{5,21},{6,22},{7,23},{8,24},{9,... | collective-permute-start | bytes 147464 | tf_op jit(solution)/shard_map/ppermute | solution.py:329
  21.3 6.1 %collective-permute-start.7 = (bf16[32,768]{1,0:T(8,128)(2,1)S(1)}, bf16[32,768]{1,0:T(8,128)(2,1)S(1)}, u32[]{:S(2)}, u32[]{:S(2)}) collective-permute-start(bf16[32,768]{1,0:T(8,128)(2,1)S(1)} %get-tuple-element.29), channel_id=1, source_target_pairs={{0,8},{1,9},{2,10},{3,11},{4,12},{5,13},{6,14},{7,15},{8,0},{9,1},... | collective-permute-start | bytes 147464 | tf_op jit(solution)/shard_map/ppermute | solution.py:329
  22.0 8.4 %collective-permute-start.2 = (bf16[32,768]{1,0:T(8,128)(2,1)S(1)}, bf16[32,768]{1,0:T(8,128)(2,1)S(1)}, u32[]{:S(2)}, u32[]{:S(2)}) collective-permute-start(bf16[32,768]{1,0:T(8,128)(2,1)S(1)} %unit.1), channel_id=1, source_target_pairs={{0,24},{1,25},{2,26},{3,27},{4,28},{5,29},{6,30},{7,31},{8,16},{9,... | collective-permute-start | bytes 147464 | tf_op jit(solution)/shard_map/ppermute | solution.py:329
  25.8 5.2 %collective-permute-start.1 = (bf16[32,768]{1,0:T(8,128)(2,1)S(1)}, bf16[32,768]{1,0:T(8,128)(2,1)S(1)}, u32[]{:S(2)}, u32[]{:S(2)}) collective-permute-start(bf16[32,768]{1,0:T(8,128)(2,1)S(1)} %unit.1), channel_id=1, source_target_pairs={{0,16},{1,17},{2,18},{3,19},{4,20},{5,21},{6,22},{7,23},{8,24},{9,... | collective-permute-start | bytes 147464 | tf_op jit(solution)/shard_map/ppermute | solution.py:329
  25.8 5.2 %collective-permute-start = (bf16[32,768]{1,0:T(8,128)(2,1)S(1)}, bf16[32,768]{1,0:T(8,128)(2,1)S(1)}, u32[]{:S(2)}, u32[]{:S(2)}) collective-permute-start(bf16[32,768]{1,0:T(8,128)(2,1)S(1)} %unit.1), channel_id=1, source_target_pairs={{0,8},{1,9},{2,10},{3,11},{4,12},{5,13},{6,14},{7,15},{8,0},{9,1},... | collective-permute-start | bytes 147464 | tf_op jit(solution)/shard_map/ppermute | solution.py:329
  27.4 8.8 %collective-permute-start.12 = (bf16[128,768]{1,0:T(8,128)(2,1)S(1)}, bf16[128,768]{1,0:T(8,128)(2,1)S(1)}, u32[]{:S(2)}, u32[]{:S(2)}) collective-permute-start(bf16[128,768]{1,0:T(8,128)(2,1)S(1)} %constant_dynamic-update-slice_fusion.8), channel_id=1, source_target_pairs={{0,6},{1,7},{2,4},{3,5},{4,2},{5,3},{6,0},{7,1},{8,14},{9,15},{10,... | collective-permute-start | bytes 589832 | tf_op jit(solution)/shard_map/ppermute | solution.py:329
  29.9 11.9 %collective-permute-start.11 = (bf16[128,768]{1,0:T(8,128)(2,1)S(1)}, bf16[128,768]{1,0:T(8,128)(2,1)S(1)}, u32[]{:S(2)}, u32[]{:S(2)}) collective-permute-start(bf16[128,768]{1,0:T(8,128)(2,1)S(1)} %constant_dynamic-update-slice_fusion.8), channel_id=1, source_target_pairs={{0,4},{1,5},{2,6},{3,7},{4,0},{5,1},{6,2},{7,3},{8,12},{9,13},{10,... | collective-permute-start | bytes 589832 | tf_op jit(solution)/shard_map/ppermute | solution.py:329
  30.4 11.4 %collective-permute-start.10 = (bf16[128,768]{1,0:T(8,128)(2,1)S(1)}, bf16[128,768]{1,0:T(8,128)(2,1)S(1)}, u32[]{:S(2)}, u32[]{:S(2)}) collective-permute-start(bf16[128,768]{1,0:T(8,128)(2,1)S(1)} %constant_dynamic-update-slice_fusion.8), channel_id=1, source_target_pairs={{0,2},{1,3},{2,0},{3,1},{4,6},{5,7},{6,4},{7,5},{8,10},{9,11},{10,... | collective-permute-start | bytes 589832 | tf_op jit(solution)/shard_map/ppermute | solution.py:329
  31.1 13.0 %collective-permute-start.5 = (bf16[128,768]{1,0:T(8,128)(2,1)S(1)}, bf16[128,768]{1,0:T(8,128)(2,1)S(1)}, u32[]{:S(2)}, u32[]{:S(2)}) collective-permute-start(bf16[128,768]{1,0:T(8,128)(2,1)S(1)} %constant_dynamic-update-slice_fusion), channel_id=1, source_target_pairs={{0,6},{1,7},{2,4},{3,5},{4,2},{5,3},{6,0},{7,1},{8,14},{9,15},{10,... | collective-permute-start | bytes 589832 | tf_op jit(solution)/shard_map/ppermute | solution.py:329
  33.5 12.2 %collective-permute-start.4 = (bf16[128,768]{1,0:T(8,128)(2,1)S(1)}, bf16[128,768]{1,0:T(8,128)(2,1)S(1)}, u32[]{:S(2)}, u32[]{:S(2)}) collective-permute-start(bf16[128,768]{1,0:T(8,128)(2,1)S(1)} %constant_dynamic-update-slice_fusion), channel_id=1, source_target_pairs={{0,4},{1,5},{2,6},{3,7},{4,0},{5,1},{6,2},{7,3},{8,12},{9,13},{10,... | collective-permute-start | bytes 589832 | tf_op jit(solution)/shard_map/ppermute | solution.py:329
  36.3 9.6 %collective-permute-start.3 = (bf16[128,768]{1,0:T(8,128)(2,1)S(1)}, bf16[128,768]{1,0:T(8,128)(2,1)S(1)}, u32[]{:S(2)}, u32[]{:S(2)}) collective-permute-start(bf16[128,768]{1,0:T(8,128)(2,1)S(1)} %constant_dynamic-update-slice_fusion), channel_id=1, source_target_pairs={{0,2},{1,3},{2,0},{3,1},{4,6},{5,7},{6,4},{7,5},{8,10},{9,11},{10,... | collective-permute-start | bytes 589832 | tf_op jit(solution)/shard_map/ppermute | solution.py:329
  46.0 2.4 %collective-permute-start.13 = (bf16[512,768]{1,0:T(8,128)(2,1)S(1)}, bf16[512,768]{1,0:T(8,128)(2,1)S(1)}, u32[]{:S(2)}, u32[]{:S(2)}) collective-permute-start(bf16[512,768]{1,0:T(8,128)(2,1)S(1)} %constant_dynamic-update-slice_fusion.12.texts_a), channel_id=1, source_target_pairs={{0,1},{1,0},{2,3},{3,2},{4,5},{5,4},{6,7},{7,6},{8,9},{9,8},{10,11... | collective-permute-start | bytes 2359304 | tf_op jit(solution)/shard_map/ppermute | solution.py:329
  46.1 3.3 %collective-permute-start.6 = (bf16[512,768]{1,0:T(8,128)(2,1)S(1)}, bf16[512,768]{1,0:T(8,128)(2,1)S(1)}, u32[]{:S(2)}, u32[]{:S(2)}) collective-permute-start(bf16[512,768]{1,0:T(8,128)(2,1)S(1)} %constant_dynamic-update-slice_fusion.4.images_a), channel_id=1, source_target_pairs={{0,1},{1,0},{2,3},{3,2},{4,5},{5,4},{6,7},{7,6},{8,9},{9,8},{10,11... | collective-permute-start | bytes 2359304 | tf_op jit(solution)/shard_map/ppermute | solution.py:329
